TPU v7x, 32 devices: a whole 2x2x4 slice. The times are simulated.
32 devices in a mesh: ens: 2 (over y), box: 4 (over z), slab: 4 (over x, core).
Axes of the slice: x: 2, y: 2, z: 4, core: 2. Of those that a mesh axis runs over, the one named last changes fastest.
Arguments:
- pressure_now: float32 [4, 64, 64, 256], P('ens', 'box', 'slab'), parts along dimension 0, may hold values from -6 to 6
- pressure_prev: float32 [4, 64, 64, 256], P('ens', 'box', 'slab'), parts along dimension 0, may hold values from -6 to 6
- courant_sq: float32 [64, 64, 256], P('box', 'slab'), may hold values from 0.04 to 0.28
- member_profiles: float32 [8, 64], replicated, may hold values from -0.15 to 0.15
- member_ids: int32 [4], P('ens'), parts along dimension 0, may hold values from 0 to 7, as said below
- stored_slabs: float32 [8, 16, 6144], P('slab'), may hold values from -6 to 6
- slab_home: int32 [2], P('ens'), parts along dimension 0, may hold values from 0 to 7
- interp_weights: float32 [2, 16], replicated, may hold values from -1.5 to 1.5
- surface_cells: int32 [6, 1024], replicated, may hold values from 0 to 1048575, as said below
Outputs:
- pressure_next: float32 [4, 64, 64, 256], P('ens', 'box', 'slab'), parts along dimension 0
- pressure_last: float32 [4, 64, 64, 256], P('ens', 'box', 'slab'), parts along dimension 0
There are 2 independent parts, one for each index of `ens`. A program takes and returns all parts, laid end to end along the dimension named above; an argument that names none is the same for every part. Nothing has to cross between parts.
Inputs may be any that keep to these rules, and one draw needn't show every extreme that they name: `surface_cells`: row f lists 1024 cells, flat index (x 64 + z) * 256 + y, on one face of the box surface 0 cells inside the grid: x low, x high, z low, z high, y low, y high in this order; the other two coordinates lie on the surface; on every face other than the two depth faces, every depth of the surface occurs; cells may repeat. `slab_home`: block k is stored on the slab device k // 2, in its slot k % 2. `member_ids`: the members' profiles are all different.
All inputs are finite; a program needn't handle non-finite values.
Results may differ from a plain program's by a relative error of at most 0.000098.
Values sent between devices are 32-bit elements; how exact they have to be, the bound alone decides.
No kernel may reach another device: no remote copies, remote signals or barrier semaphores. Data moves between devices by JAX's collectives and lax.ppermute only.
A program may use at most 64 MiB of HBM per device.

v0:
```python
import functools

import jax
import jax.numpy as jnp
from jax import lax
from jax.experimental import pallas as pl
from jax.experimental.pallas import tpu as pltpu
from jax.sharding import PartitionSpec as P


F32 = jnp.float32
BF16 = jnp.bfloat16
VMEM = pl.BlockSpec(memory_space=pltpu.VMEM)
SMEM = pl.BlockSpec(memory_space=pltpu.SMEM)
HBM = pl.BlockSpec(memory_space=pl.ANY)
CORNERS = 8
PARAMS = pltpu.CompilerParams(vmem_limit_bytes=16 * 1024 * 1024)


LANES = 128
STRIP = 8


def rows_of(shape, axis):
    return lax.broadcasted_iota(jnp.int32, shape, axis)


def up16(n):
    return (n + 15) // 16 * 16


def beside_y(tiles):
    lane = rows_of(tiles[0].shape, 1)
    right = [pltpu.roll(t, 1, 1) for t in tiles]
    left = [pltpu.roll(t, LANES - 1, 1) for t in tiles]
    before = [0.0] + right[:-1]
    after = left[1:] + [0.0]
    return [
        jnp.where(lane == 0, b, r) + jnp.where(lane == LANES - 1, a, l)
        for b, r, l, a in zip(before, right, left, after)
    ]


def beside_rows(tile, low, high):
    strips = [tile[i : i + STRIP] for i in range(0, tile.shape[0], STRIP)]
    row = rows_of(strips[0].shape, 0)
    down = [pltpu.roll(t, 1, 0) for t in strips]
    up = [pltpu.roll(t, STRIP - 1, 0) for t in strips]
    below = [low] + down[:-1]
    above = up[1:] + [high]
    sums = [
        jnp.where(row == 0, b, d) + jnp.where(row == STRIP - 1, a, u)
        for b, d, u, a in zip(below, down, up, above)
    ]
    return jnp.concatenate(sums, axis=0)


def halves(ref):
    return range(ref.shape[0])


def lanes(h):
    return slice(h * LANES, (h + 1) * LANES)


def depth_rows(ref, z, *lead):
    width_x, width_z = ref.shape[-3:-1]
    count = 1
    for n in ref.shape[:-3]:
        count = count * n
    at = 0
    for i, n in zip(lead, ref.shape[:-3]):
        at = at * n + i
    flat = ref.reshape(count * width_x * width_z, LANES)
    return flat[pl.ds(at * width_x * width_z + z, width_x, stride=width_z), :]


def pack_kernel(
    slots, home, ids_in, weights_in, prof_in, now_in, prev_in, cour_in, cells_in, slabs,
    now, prev, cour, cells, planes, edges, za, zb, vals, xa, xb, ids, weights, prof, block, sems,
):
    _, members, width_x, width_z, _ = now.shape
    steps, samples = weights.shape
    box, slab = lax.axis_index("box"), lax.axis_index("slab")
    total_z = prof.shape[1]
    pairs = [(ids_in, ids), (prof_in, prof), (weights_in, weights)]
    for h in halves(now):
        pairs.append((now_in.at[:, :, :, pl.ds(h * LANES, LANES)], now.at[h]))
    for h in halves(now):
        pairs.append((cour_in.at[:, :, pl.ds(h * LANES, LANES)], cour.at[h]))
        pairs.append((prev_in.at[:, :, :, pl.ds(h * LANES, LANES)], prev.at[h]))
    fields = len(pairs)
    pairs.append((slabs.at[lax.rem(home[0], slots)], block))
    pairs.append((cells_in, cells))
    loads = [pltpu.make_async_copy(a, b, sems.at[i]) for i, (a, b) in enumerate(pairs)]
    for load in loads:
        load.start()
    start_z = slab * width_z
    for load in loads[:3]:
        load.wait()
    row = rows_of((width_z, LANES), 0)
    for m in range(members):
        plane = jnp.zeros((width_z, LANES), F32)
        for z in range(width_z):
            plane = jnp.where(row == z, 1.0 + prof[ids[m], start_z + z], plane)
        planes[m] = plane
        for s, z in ((0, start_z - 1), (1, start_z + width_z)):
            beyond = 1.0 + prof[ids[m], jnp.clip(z, 0, total_z - 1)]
            edges[2 * m + s : 2 * m + s + 1] = jnp.full((1, LANES), beyond, F32)
    owner = slab == home[0] // slots
    points = block.shape[1]
    width = vals.shape[1]
    chunks = points // width
    sample = rows_of((samples, width), 0)
    columns = []
    for t in range(steps):
        column = jnp.zeros((samples, width), F32)
        for k in range(samples):
            column = jnp.where(sample == k, weights[t, k], column)
        columns.append(jnp.where(owner, column, 0.0))
    zero = jnp.zeros((1, LANES), F32)
    for load in loads[3:fields]:
        load.wait()
    face, side = lax.rem(box, 2), lax.rem(slab, 2)

    def local_step(heres, prevs, inners, coefs):
        near = beside_y(heres)
        out = []
        for here, prev_here, inner, coef, n in zip(heres, prevs, inners, coefs, near):
            around = n + beside_rows(here, zero, zero) + inner
            out.append(2.0 * here - prev_here + coef * (around - 6.0 * here))
        return out

    for a, b, at_high, get, length in (
        (za, zb, side == 0, "z", width_z),
        (xa, xb, face == 0, "x", width_x),
    ):
        ends = []
        for at, inner in ((0, 1), (length - 1, length - 2)):
            parts = [[] for _ in halves(now)]
            if get == "x":
                courant = [cour[h, at] for h in halves(now)]
            else:
                courant = [depth_rows(cour, at, h) for h in halves(now)]
            steps_here = []
            for m in range(members):
                if get == "x":
                    heres, prevs, inners = (
                        [ref[h, m, i] for h in halves(now)]
                        for ref, i in ((now, at), (prev, at), (now, inner))
                    )
                    coefs = [c * planes[m] for c in courant]
                else:
                    heres, prevs, inners = (
                        [depth_rows(ref, i, h, m) for h in halves(now)]
                        for ref, i in ((now, at), (prev, at), (now, inner))
                    )
                    coefs = [c * (1.0 + prof[ids[m], start_z + at]) for c in courant]
                steps_here.append(local_step(heres, prevs, inners, coefs))
                for h in halves(now):
                    parts[h].append(heres[h])
            for h in halves(now):
                ends.append(parts[h] + [r[h] for r in steps_here] + [courant[h]])
        count = len(ends) // 2
        for h in range(count):
            for i, (low, high) in enumerate(zip(ends[h], ends[count + h])):
                n = low.shape[0]
                a[i * n : (i + 1) * n, lanes(h)] = jnp.where(at_high, high, low)
                b[i * n : (i + 1) * n, lanes(h)] = jnp.where(at_high, low, high)
    loads[fields].wait()
    for c in range(chunks):
        piece = block[:, c * width : (c + 1) * width]
        for t in range(steps):
            at = t * chunks + c
            vals[at : at + 1] = jnp.sum(columns[t] * piece, axis=0, keepdims=True)
    loads[fields + 1].wait()
    tail = (2 * members + 1) * width_x
    offered = vals[...]
    zb[tail:] = offered


def relay_kernel(relay, face, vals, zb, after, za):
    tail = face.shape[0]
    za[:tail] = face[...]
    za[tail:] = vals[...] + zb[tail:] if relay else vals[...]


def corner_kernel(members, width_z, xa, xb, after, ca, cb):
    box, slab = lax.axis_index("box"), lax.axis_index("slab")
    face, side = lax.rem(box, 2), lax.rem(slab, 2)
    for out, last in ((ca, side == 0), (cb, side == 1)):
        for m in range(members):
            lo, hi = m * width_z, (m + 1) * width_z - 1
            a = jnp.where(last, xa[hi : hi + 1], xa[lo : lo + 1])
            b = jnp.where(last, xb[hi : hi + 1], xb[lo : lo + 1])
            out[2 * m : 2 * m + 1] = jnp.where(face == 0, b, a)
            out[2 * m + 1 : 2 * m + 2] = jnp.where(face == 0, a, b)


def split_cell(cell, total_z, depth_y):
    plane = total_z * depth_y
    x = cell // plane
    rest = cell - x * plane
    z = rest // depth_y
    return x, z, rest - z * depth_y


def extended_row(coordinate, start, width):
    d = coordinate - start
    edge = jnp.where(d == -1, width, jnp.where(d == width, width + 1, -1))
    return jnp.where((d >= 0) & (d < width), d, edge)


def one_hot(index, high):
    rows = rows_of((high, index.shape[1]), 0)
    return jnp.where(rows == index, 1.0, 0.0).astype(BF16)


def faces_of(box, slab):
    return jnp.where(box == 0, 0, 1), jnp.where(slab == 0, 2, 3), 4, 5


def local_kernel(
    boxes, slabs, total_z, planes, cells, now, prev, cour, local, wide, narrow, rows_x, rows_z,
):
    count, members, width_x, width_z, _ = now.shape
    depth_y = count * LANES
    box, slab = lax.axis_index("box"), lax.axis_index("slab")
    zero = jnp.zeros((1, LANES), F32)
    for x in range(width_x):
        for m in range(members):
            heres = [now[h, m, x] for h in range(count)]
            near = beside_y(heres)
            for h, here in enumerate(heres):
                around = near[h] + beside_rows(here, zero, zero)
                if x > 0:
                    around = around + now[h, m, x - 1]
                if x < width_x - 1:
                    around = around + now[h, m, x + 1]
                coef = cour[h, x] * planes[m]
                local[h, m, x] = 2.0 * here - prev[h, m, x] + coef * (around - 6.0 * here)
    on_x = (box == 0) | (box == boxes - 1)
    on_z = (slab == 0) | (slab == slabs - 1)
    for i, f in enumerate(faces_of(box, slab)):
        x, z, y = split_cell(cells[pl.ds(f, 1), :], total_z, depth_y)
        x = extended_row(x, box * width_x, width_x)
        z = extended_row(z, slab * width_z, width_z)
        if i == 0:
            rows_z[0] = one_hot(jnp.where(on_x, z, -1), rows_z.shape[1])
            wide[0] = one_hot(y, depth_y)
        elif i == 1:
            rows_x[...] = one_hot(jnp.where(on_z, x, -1), rows_x.shape[0])
            wide[1] = one_hot(y, depth_y)
        else:
            rows_z[i - 1] = one_hot(z, rows_z.shape[1])
            narrow[i - 2] = one_hot(x, narrow.shape[1])


def three_parts(v):
    first = v.astype(BF16)
    rest = v - first.astype(F32)
    second = rest.astype(BF16)
    third = (rest - second.astype(F32)).astype(BF16)
    return first, second, third


def face_source(values, rows, rhs, width):
    heights = [rows.shape[0]] + [up16(width)] * (len(values) - 1)
    parts = []
    for v, high in zip(values, heights):
        for part in three_parts(v):
            parts.append(rows[:high] * jnp.broadcast_to(part, (high, part.shape[1])))
    out = lax.dot_general(
        jnp.concatenate(parts, axis=0), rhs, (((1,), (1,)), ((), ())), preferred_element_type=F32
    )
    sums, at = [], 0
    for high in heights:
        one, two, three = (out[at + i * high : at + (i + 1) * high] for i in range(3))
        sums.append((three + two) + one)
        at = at + 3 * high
    return sums


def main_kernel(
    boxes, slabs, received, planes, edges, wide, narrow, rows_x, rows_z, now, local, cour,
    vals, za, zb, xa, xb, *rest,
):
    others, rest = rest[:received], rest[received:]
    one, nxt, late, hz, xlo, xhi, zlo, zhi, value, xsrc, zsrc = rest
    count, members, width_x, width_z, _ = now.shape
    depth_y = count * LANES
    box, slab = lax.axis_index("box"), lax.axis_index("slab")
    face, side = lax.rem(box, 2), lax.rem(slab, 2)
    span_z = (2 * members + 1) * width_x
    low, high = (box > 0, slab > 0), (box < boxes - 1, slab < slabs - 1)
    xlo[...] = jnp.where(low[0], jnp.where(face == 0, xb[...], xa[...]), 0.0)
    xhi[...] = jnp.where(high[0], jnp.where(face == 0, xa[...], xb[...]), 0.0)
    zlo[...] = jnp.where(low[1], jnp.where(side == 0, zb[:span_z], za[:span_z]), 0.0)
    zhi[...] = jnp.where(high[1], jnp.where(side == 0, za[:span_z], zb[:span_z]), 0.0)
    total = vals[...] + za[span_z:]
    if slabs == 4:
        total = total + zb[span_z:]
    for other in others:
        total = total + other[...]
    value[...] = total

    steps = xsrc.shape[0]
    chunks = value.shape[0] // steps
    per = wide.shape[2] // depth_y
    faces = faces_of(box, slab)

    def of_face(f):
        vs = []
        for t in range(steps):
            pieces = [value[pl.ds(t * chunks + f * per + i, 1), :] for i in range(per)]
            vs.append(jnp.concatenate(pieces, axis=1))
        return vs

    for t, s in enumerate(face_source(of_face(faces[0]), rows_z[0], wide[0], width_z)):
        xsrc[t, : s.shape[0]] = s
    for t, s in enumerate(face_source(of_face(faces[1]), rows_x[...], wide[1], width_x)):
        zsrc[t, : s.shape[0]] = s
    ys = [
        face_source(of_face(faces[2 + i]), rows_z[1 + i], narrow[i], width_z) for i in range(2)
    ]

    lane = rows_of((width_z, LANES), 1)
    row = rows_of((width_z, LANES), 0)
    row_of_z = jnp.where(slab == 0, 0, jnp.where(slab == slabs - 1, width_z - 1, -1))
    row_of_x = jnp.where(box == 0, 0, jnp.where(box == boxes - 1, width_x - 1, -1))

    def plane_source(t, x):
        out = []
        for h in range(count):
            part = jnp.where(row == row_of_z, zsrc[t, x : x + 1, lanes(h)], 0.0)
            if h == 0:
                part = part + jnp.where(lane == 0, ys[0][t][:width_z, x : x + 1], 0.0)
            if h == count - 1:
                part = part + jnp.where(lane == LANES - 1, ys[1][t][:width_z, x : x + 1], 0.0)
            if x in (0, width_x - 1):
                part = part + jnp.where(row_of_x == x, xsrc[t, :width_z, lanes(h)], 0.0)
            out.append(part)
        return out

    lane_x = rows_of((width_x, LANES), 1)
    row_x = rows_of((width_x, LANES), 0)
    turned = [jnp.transpose(y[0]) for y in ys]

    def row_source(z):
        out = []
        for h in range(count):
            part = jnp.where(row_x == row_of_x, xsrc[0, z : z + 1, lanes(h)], 0.0)
            if h == 0:
                part = part + jnp.where(lane_x == 0, turned[0][:width_x, z : z + 1], 0.0)
            if h == count - 1:
                part = part + jnp.where(lane_x == LANES - 1, turned[1][:width_x, z : z + 1], 0.0)
            out.append(part)
        return out

    side_x, side_z = 2 * members * width_z, 2 * members * width_x
    halo_x, coef_x, coef_z = {}, {}, {}
    for s, (ref, x) in enumerate(((xlo, 0), (xhi, width_x - 1))):
        source = plane_source(0, width_x + s)
        for m in range(members):
            for h in range(count):
                coef = ref[side_x:, lanes(h)] * planes[m]
                base = ref[(members + m) * width_z : (members + m + 1) * width_z, lanes(h)]
                halo_x[s, m, h] = base + coef * now[h, m, x] + source[h]
                coef_x[s, m, h] = coef
    for s, (ref, z) in enumerate(((zlo, 0), (zhi, width_z - 1))):
        source = row_source(width_z + s)
        for m in range(members):
            for h in range(count):
                coef = ref[side_z:, lanes(h)] * edges[2 * m + s : 2 * m + s + 1]
                base = ref[(members + m) * width_x : (members + m + 1) * width_x, lanes(h)]
                hz[s, h, m] = base + coef * depth_rows(now, z, h, m) + source[h]
                coef_z[s, m, h] = coef
    for x in range(width_x):
        source = plane_source(0, x)
        for m in range(members):
            at = m * width_x + x
            for h in range(count):
                low_row, high_row = zlo[at : at + 1, lanes(h)], zhi[at : at + 1, lanes(h)]
                more = jnp.where(row == 0, low_row, jnp.where(row == width_z - 1, high_row, 0.0))
                if x == 0:
                    more = more + xlo[m * width_z : (m + 1) * width_z, lanes(h)]
                if x == width_x - 1:
                    more = more + xhi[m * width_z : (m + 1) * width_z, lanes(h)]
                one[h, m, x] = local[h, m, x] + (cour[h, x] * planes[m]) * more + source[h]
    for x in range(width_x):
        source = plane_source(1, x)
        for m in range(members):
            heres = [one[h, m, x] for h in range(count)]
            near = beside_y(heres)
            for h, here in enumerate(heres):
                rows = beside_rows(here, hz[0, h, m, x : x + 1], hz[1, h, m, x : x + 1])
                around = near[h] + rows
                around = around + (one[h, m, x - 1] if x > 0 else halo_x[0, m, h])
                around = around + (one[h, m, x + 1] if x < width_x - 1 else halo_x[1, m, h])
                coef = cour[h, x] * planes[m]
                nxt[h, m, x] = 2.0 * here - now[h, m, x] + coef * (around - 6.0 * here) + source[h]
                if x in (0, width_x - 1):
                    s = 0 if x == 0 else 1
                    for e, z in ((0, 0), (1, width_z - 1)):
                        beyond = coef_z[e, m, h][x : x + 1] + coef_x[s, m, h][z : z + 1]
                        at = 2 * (members * e + m) + s
                        late[at : at + 1, lanes(h)] = coef[z : z + 1] * beyond


def fix_kernel(boxes, slabs, ca, cb, one, nxt, late, out, last, done, sems):
    count, members, width_x, width_z, _ = nxt.shape
    box, slab = lax.axis_index("box"), lax.axis_index("slab")
    side = lax.rem(slab, 2)
    open_x = (box > 0, box < boxes - 1)
    open_z = (slab > 0, slab < slabs - 1)
    row = rows_of((width_z, LANES), 0)
    copies = []

    def send(source, target):
        copies.append(pltpu.make_async_copy(source, target, sems.at[len(copies)]))
        copies[-1].start()

    for h in range(count):
        inside = pl.ds(1, width_x - 2)
        for m in range(members):
            send(nxt.at[h, m, inside], out.at[m, inside, :, pl.ds(h * LANES, LANES)])
            send(one.at[h, m], last.at[m, :, :, pl.ds(h * LANES, LANES)])
    for h in range(count):
        for m in range(members):
            for s, x in ((0, 0), (1, width_x - 1)):
                at = 2 * m + s
                add = 0.0
                for e, z in ((0, 0), (1, width_z - 1)):
                    got = jnp.where(
                        side == e, cb[at : at + 1, lanes(h)], ca[at : at + 1, lanes(h)]
                    )
                    got = jnp.where(open_x[s] & open_z[e], got, 0.0)
                    k = 2 * members * e + at
                    add = jnp.where(row == z, late[k : k + 1, lanes(h)] * got, add)
                done[h, s, m] = nxt[h, m, x] + add
                send(done.at[h, s, m], out.at[m, x, :, pl.ds(h * LANES, LANES)])
    for copy in copies:
        copy.wait()


def pairs_even(n):
    return [i ^ 1 for i in range(n)]


def pairs_odd(n):
    return [(i + 1) % n if i % 2 else (i - 1) % n for i in range(n)]


def on_device(
    boxes, slabs, pressure_now, pressure_prev, courant_sq, member_profiles, member_ids,
    stored_slabs, slab_home, interp_weights, surface_cells,
):
    members, width_x, width_z, depth_y = pressure_now.shape
    slots, samples, points = stored_slabs.shape
    steps = interp_weights.shape[0]
    total_z = width_z * slabs
    value_rows = steps * points // depth_y
    span_x = (2 * members + 1) * width_z
    span_z = (2 * members + 1) * width_x
    count = depth_y // LANES

    def inner(*dims, dtype=F32):
        return pltpu.VMEM(dims, dtype)

    def far(*arrays):
        return [pltpu.with_memory_space_constraint(a, pltpu.HBM) for a in arrays]

    def near(*arrays):
        return [pltpu.with_memory_space_constraint(a, pltpu.VMEM) for a in arrays]

    def over_slab(x, partner):
        return lax.ppermute(x, "slab", list(enumerate(partner)))

    def over_box(x, odd):
        pairs = []
        for b in range(boxes):
            other = b ^ 1
            if odd:
                other = b + 1 if b % 2 else b - 1
            for s in range(slabs):
                inside = 0 <= other < boxes
                to = other * slabs + s if inside else b * slabs + (s ^ 1)
                pairs.append((b * slabs + s, to))
        return lax.ppermute(x, ("box", "slab"), pairs)

    whole = pressure_now.shape
    half = (count,) + whole[:3] + (LANES,)
    now, prev, cour, cells, planes, edges, za, zb, vals, xa, xb = pl.pallas_call(
        functools.partial(pack_kernel, slots),
        out_shape=(
            inner(*half),
            inner(*half),
            inner(count, width_x, width_z, LANES),
            inner(*surface_cells.shape, dtype=jnp.int32),
            inner(members, width_z, LANES),
            inner(2 * members, LANES),
            inner(span_z, depth_y),
            inner(span_z + value_rows, depth_y),
            inner(value_rows, depth_y),
            inner(span_x, depth_y),
            inner(span_x, depth_y),
        ),
        in_specs=[SMEM] + [HBM] * 8,
        out_specs=(VMEM,) * 11,
        scratch_shapes=[
            pltpu.SMEM(member_ids.shape, jnp.int32),
            pltpu.SMEM(interp_weights.shape, F32),
            pltpu.SMEM(member_profiles.shape, F32),
            pltpu.VMEM((samples, points), F32),
            pltpu.SemaphoreType.DMA((5 + 3 * count,)),
        ],
        compiler_params=PARAMS,
        name="pack",
    )(
        slab_home, *far(member_ids, interp_weights, member_profiles),
        *far(pressure_now, pressure_prev, courant_sq, surface_cells, stored_slabs),
    )

    per_face = surface_cells.shape[1]
    zb = over_slab(zb, pairs_odd(slabs))
    xa = over_box(xa, False)
    xb = over_box(xb, True)
    others = [
        over_slab(vals, [i ^ k for i in range(slabs)])
        for k in range(2, slabs)
        if slabs != 4
    ]
    now, prev, cour, cells, vals, planes, edges = near(
        now, prev, cour, cells, vals, planes, edges
    )
    high_x, high_z = up16(width_x + 2), up16(width_z + 2)
    local, wide, narrow, rows_x, rows_z = near(
        *pl.pallas_call(
            functools.partial(local_kernel, boxes, slabs, total_z),
            out_shape=(
                inner(*half),
                inner(2, depth_y, per_face, dtype=BF16),
                inner(2, high_x, per_face, dtype=BF16),
                inner(high_x, per_face, dtype=BF16),
                inner(3, high_z, per_face, dtype=BF16),
            ),
            in_specs=[VMEM] * 5,
            out_specs=(VMEM,) * 5,
            compiler_params=PARAMS,
            name="local",
        )(planes, cells, now, prev, cour)
    )
    za, zb, xa, xb, *others = near(za, zb, xa, xb, *others)
    za = pl.pallas_call(
        functools.partial(relay_kernel, slabs == 4),
        out_shape=inner(span_z + value_rows, depth_y),
        in_specs=[VMEM] * 4,
        out_specs=VMEM,
        compiler_params=PARAMS,
        name="relay",
    )(za, vals, zb, local)
    ca, cb = pl.pallas_call(
        functools.partial(corner_kernel, members, width_z),
        out_shape=(inner(CORNERS, depth_y),) * 2,
        in_specs=[VMEM] * 3,
        out_specs=(VMEM, VMEM),
        compiler_params=PARAMS,
        name="corner",
    )(xa, xb, *near(za))
    za = over_slab(za, pairs_even(slabs))
    ca = over_slab(ca, pairs_even(slabs))
    cb = over_slab(cb, pairs_odd(slabs))
    za, ca, cb = near(za, ca, cb)

    one, nxt, late = pl.pallas_call(
        functools.partial(main_kernel, boxes, slabs, len(others)),
        out_shape=(inner(*half), inner(*half), inner(4 * members, depth_y)),
        in_specs=[VMEM] * (14 + len(others)),
        out_specs=(VMEM, VMEM, VMEM),
        scratch_shapes=[
            inner(2, count, members, width_x, LANES),
            inner(span_x, depth_y),
            inner(span_x, depth_y),
            inner(span_z, depth_y),
            inner(span_z, depth_y),
            inner(value_rows, depth_y),
            inner(steps, high_z, depth_y),
            inner(steps, high_x, depth_y),
        ],
        compiler_params=PARAMS,
        name="main",
    )(
        planes, edges, wide, narrow, rows_x, rows_z, now, local, cour,
        vals, za, zb, xa, xb, *others,
    )
    return pl.pallas_call(
        functools.partial(fix_kernel, boxes, slabs),
        out_shape=(pltpu.HBM(whole, F32),) * 2,
        in_specs=[VMEM] * 5,
        out_specs=(HBM, HBM),
        scratch_shapes=[
            inner(count, 2, members, width_z, LANES),
            pltpu.SemaphoreType.DMA((4 * count * members,)),
        ],
        compiler_params=PARAMS,
        name="fix",
    )(ca, cb, *near(one, nxt, late))


def solution(mesh):
    in_specs = (
        P("ens", "box", "slab", None),
        P("ens", "box", "slab", None),
        P("box", "slab", None),
        P(),
        P("ens"),
        P("slab", None, None),
        P("ens"),
        P(),
        P(),
    )
    out_specs = (P("ens", "box", "slab", None), P("ens", "box", "slab", None))
    boxes, slabs = mesh.shape["box"], mesh.shape["slab"]
    return jax.shard_map(
        functools.partial(on_device, boxes, slabs),
        mesh=mesh,
        in_specs=in_specs,
        out_specs=out_specs,
        check_vma=False,
    )
```

profile of v0, /device:TPU:19, one launch (start us, length us, event | category | flops | bytes accessed | tf_op | source)
XLA Modules:
  0.0 20.0 jit_solution(5657382748074770159)
XLA Ops:
  1.3 1.7 %pack.1 = (f32[2,2,16,16,128]{4,3,2,1,0:T(8,128)S(1)}, f32[2,2,16,16,128]{4,3,2,1,0:T(8,128)S(1)}, f32[2,16,16,128]{3,2,1,0:T(8,128)S(1)}, s32[6,1024]{1,0:T(8,1...) custom-call(s32[1]{0:T(128)S(6)} %copy.11.home, ...), custom_call_target="tpu_custom_call" | custom-call | tf_op jit(solution)/shard_map/pack/pallas_call | solution.py:493
  3.0 0.9 %collective-permute-start.2 = (f32[128,256]{1,0:T(8,128)S(1)}, f32[128,256]{1,0:T(8,128)S(1)}, u32[]{:S(2)}, u32[]{:S(2)}) collective-permute-start(f32[128,256]{1,0:T(8,128)S(1)} %get-tuple-element.27), channel_id=1, source_target_pairs={{0,3},{1,2},{2,1},{3,0},{4,7},{5,6},{6,5},{7,4},{8,11},{9,10},{10,... | collective-permute-start | bytes 393224 | tf_op jit(solution)/shard_map/ppermute | solution.py:477
  3.9 1.0 %local.1 = (f32[2,2,16,16,128]{4,3,2,1,0:T(8,128)S(1)}, bf16[2,256,1024]{2,1,0:T(8,128)(2,1)S(1)}, bf16[2,32,1024]{2,1,0:T(8,128)(2,1)S(1)}, bf16[32,1024]{1,0:T(8,128)(2,1)S(1)}, bf16[3,32,1024]{2,1,0:T(8,128)(2,1)S(1)}) custom-call(f32[2,16,128]{2,1,0:T(8,128)S(1)} %get-tuple-element.28.planes, s32[6,1024]{1,0:T(8,128)S(1)} %get-tuple-element.29.cells, ...), custom_call_target="tpu_custom_call" | custom-call | tf_op jit(solution)/shard_map/local/pallas_call | solution.py:538
  4.9 4.2 %collective-permute-done.2.zb = f32[128,256]{1,0:T(8,128)S(1)} collective-permute-done((f32[128,256]{1,0:T(8,128)S(1)}, f32[128,256]{1,0:T(8,128)S(1)}, u32[]{:S(2)}, u32[]{:S(2)}) %collective-permute-start.2) | collective-permute-done | bytes 131104 | tf_op jit(solution)/shard_map/ppermute | solution.py:477
  9.1 0.5 %collective-permute-start.5 = (f32[128,256]{1,0:T(8,128)S(1)}, f32[128,256]{1,0:T(8,128)S(1)}, u32[]{:S(2)}, u32[]{:S(2)}) collective-permute-start(f32[128,256]{1,0:T(8,128)S(1)} %relay.1.after), channel_id=1, source_target_pairs={{0,1},{1,0},{2,3},{3,2},{4,5},{5,4},{6,7},{7,6},{8,9},{9,8},{10,11... | collective-permute-start | bytes 393224 | tf_op jit(solution)/shard_map/ppermute | solution.py:477
  9.6 1.3 %collective-permute-start = (f32[80,256]{1,0:T(8,128)S(1)}, f32[80,256]{1,0:T(8,128)S(1)}, u32[]{:S(2)}, u32[]{:S(2)}) collective-permute-start(f32[80,256]{1,0:T(8,128)S(1)} %get-tuple-element.23), channel_id=1, source_target_pairs={{0,4},{1,5},{2,6},{3,7},{4,0},{5,1},{6,2},{7,3},{8,12},{9,13},{10,... | collective-permute-start | bytes 245768 | tf_op jit(solution)/shard_map/ppermute | solution.py:489
  10.9 0.0 collective-permute-start.1
  10.9 2.6 %collective-permute-done.xa = f32[80,256]{1,0:T(8,128)S(1)} collective-permute-done((f32[80,256]{1,0:T(8,128)S(1)}, f32[80,256]{1,0:T(8,128)S(1)}, u32[]{:S(2)}, u32[]{:S(2)}) %collective-permute-start) | collective-permute-done | bytes 81952 | tf_op jit(solution)/shard_map/ppermute | solution.py:489
  13.5 1.0 %collective-permute-done.1.xb = f32[80,256]{1,0:T(8,128)S(1)} collective-permute-done((f32[80,256]{1,0:T(8,128)S(1)}, f32[80,256]{1,0:T(8,128)S(1)}, u32[]{:S(2)}, u32[]{:S(2)}) %collective-permute-start.1) | collective-permute-done | bytes 81952 | tf_op jit(solution)/shard_map/ppermute | solution.py:489
  14.5 1.3 %collective-permute-start.3 = (f32[8,256]{1,0:T(8,128)S(1)}, f32[8,256]{1,0:T(8,128)S(1)}, u32[]{:S(2)}, u32[]{:S(2)}) collective-permute-start(f32[8,256]{1,0:T(8,128)S(1)} %get-tuple-element.34), channel_id=1, source_target_pairs={{0,1},{1,0},{2,3},{3,2},{4,5},{5,4},{6,7},{7,6},{8,9},{9,8},{10,11... | collective-permute-start | bytes 24584 | tf_op jit(solution)/shard_map/ppermute | solution.py:477
  15.8 0.2 collective-permute-start.4
  16.0 0.0 collective-permute-done.5.za
  16.0 1.5 %main.1 = (f32[2,2,16,16,128]{4,3,2,1,0:T(8,128)S(1)}, f32[2,2,16,16,128]{4,3,2,1,0:T(8,128)S(1)}, f32[8,256]{1,0:T(8,128)S(1)}) custom-call(f32[2,16,128]{2,1,0:T(8,128)S(1)} %get-tuple-element.28.planes, f32[4,128]{1,0:T(4,128)S(1)} %get-tuple-element.36.edges, bf16[2,256,1024]{2,1,0:T(8,128)(2,1)S(1)} %get-tuple-element.37.wide, ...), custom_call_target="tpu_custom_call" | custom-call | tf_op jit(solution)/shard_map/main/pallas_call | solution.py:575
  17.5 0.0 collective-permute-done.3.ca
  17.5 1.4 %collective-permute-done.4.cb = f32[8,256]{1,0:T(8,128)S(1)} collective-permute-done((f32[8,256]{1,0:T(8,128)S(1)}, f32[8,256]{1,0:T(8,128)S(1)}, u32[]{:S(2)}, u32[]{:S(2)}) %collective-permute-start.4) | collective-permute-done | bytes 8224 | tf_op jit(solution)/shard_map/ppermute | solution.py:477
  18.9 1.1 %fix.1 = (f32[2,16,16,256]{3,2,1,0:T(8,128)}, f32[2,16,16,256]{3,2,1,0:T(8,128)}) custom-call(f32[8,256]{1,0:T(8,128)S(1)} %collective-permute-done.3.ca, f32[8,256]{1,0:T(8,128)S(1)} %collective-permute-done.4.cb, f32[2,2,16,16,128]{4,3,2,1,0:T(8,128)S(1)} %get-tuple-element.41.one, f32[2,2,16,16,128]{4,3,2,1,0:T(8,128)S(1)} %get-tuple-element.42.nxt, ...), custom_call_target="tpu_custom_call" | custom-call | tf_op jit(solution)/shard_map/fix/pallas_call | solution.py:596
  (2 shorter events, 0.0 us)
Async XLA Ops:
  3.0 6.1 %collective-permute-start.2 = (f32[128,256]{1,0:T(8,128)S(1)}, f32[128,256]{1,0:T(8,128)S(1)}, u32[]{:S(2)}, u32[]{:S(2)}) collective-permute-start(f32[128,256]{1,0:T(8,128)S(1)} %get-tuple-element.27), channel_id=1, source_target_pairs={{0,3},{1,2},{2,1},{3,0},{4,7},{5,6},{6,5},{7,4},{8,11},{9,10},{10,... | collective-permute-start | bytes 393224 | tf_op jit(solution)/shard_map/ppermute | solution.py:477
  9.1 6.9 %collective-permute-start.5 = (f32[128,256]{1,0:T(8,128)S(1)}, f32[128,256]{1,0:T(8,128)S(1)}, u32[]{:S(2)}, u32[]{:S(2)}) collective-permute-start(f32[128,256]{1,0:T(8,128)S(1)} %relay.1.after), channel_id=1, source_target_pairs={{0,1},{1,0},{2,3},{3,2},{4,5},{5,4},{6,7},{7,6},{8,9},{9,8},{10,11... | collective-permute-start | bytes 393224 | tf_op jit(solution)/shard_map/ppermute | solution.py:477
  9.6 3.9 %collective-permute-start = (f32[80,256]{1,0:T(8,128)S(1)}, f32[80,256]{1,0:T(8,128)S(1)}, u32[]{:S(2)}, u32[]{:S(2)}) collective-permute-start(f32[80,256]{1,0:T(8,128)S(1)} %get-tuple-element.23), channel_id=1, source_target_pairs={{0,4},{1,5},{2,6},{3,7},{4,0},{5,1},{6,2},{7,3},{8,12},{9,13},{10,... | collective-permute-start | bytes 245768 | tf_op jit(solution)/shard_map/ppermute | solution.py:489
  10.9 3.6 %collective-permute-start.1 = (f32[80,256]{1,0:T(8,128)S(1)}, f32[80,256]{1,0:T(8,128)S(1)}, u32[]{:S(2)}, u32[]{:S(2)}) collective-permute-start(f32[80,256]{1,0:T(8,128)S(1)} %get-tuple-element.24), channel_id=1, source_target_pairs={{0,1},{1,0},{2,3},{3,2},{4,8},{5,9},{6,10},{7,11},{8,4},{9,5},{10,... | collective-permute-start | bytes 245768 | tf_op jit(solution)/shard_map/ppermute | solution.py:489
  14.5 3.0 %collective-permute-start.3 = (f32[8,256]{1,0:T(8,128)S(1)}, f32[8,256]{1,0:T(8,128)S(1)}, u32[]{:S(2)}, u32[]{:S(2)}) collective-permute-start(f32[8,256]{1,0:T(8,128)S(1)} %get-tuple-element.34), channel_id=1, source_target_pairs={{0,1},{1,0},{2,3},{3,2},{4,5},{5,4},{6,7},{7,6},{8,9},{9,8},{10,11... | collective-permute-start | bytes 24584 | tf_op jit(solution)/shard_map/ppermute | solution.py:477
  15.8 3.1 %collective-permute-start.4 = (f32[8,256]{1,0:T(8,128)S(1)}, f32[8,256]{1,0:T(8,128)S(1)}, u32[]{:S(2)}, u32[]{:S(2)}) collective-permute-start(f32[8,256]{1,0:T(8,128)S(1)} %get-tuple-element.35), channel_id=1, source_target_pairs={{0,3},{1,2},{2,1},{3,0},{4,7},{5,6},{6,5},{7,4},{8,11},{9,10},{10,... | collective-permute-start | bytes 24584 | tf_op jit(solution)/shard_map/ppermute | solution.py:477
where the time goes:
time: 20.2 us; the launch traced here: 20 us
  waiting for transfers between devices  9.26 us (46%)
  Pallas kernels  5.26 us (26%)
  starting transfers between devices  4.14 us (20%)
  between operations  1.32 us (7%)
    ppermute x4, waiting for transfers between devices, over_slab(): return lax.ppermute(x, 'slab', list(enumerate(partner)))  5.66 us
    ppermute x2, waiting for transfers between devices, over_box(): return lax.ppermute(x, ('box', 'slab'), pairs)  3.6 us
    ppermute x4, starting transfers between devices, over_slab(): return lax.ppermute(x, 'slab', list(enumerate(partner)))  2.84 us
    pallas_call x1, Pallas kernels, on_device(): pl.pallas_call(functools.partial(pack_kernel, slots), out_shape=(inner(*h...  1.7 us
    pallas_call x1, Pallas kernels, on_device(): pl.pallas_call(functools.partial(main_kernel, boxes, slabs, len(others)),...  1.46 us
    ppermute x2, starting transfers between devices, over_box(): return lax.ppermute(x, ('box', 'slab'), pairs)  1.3 us
    pallas_call x1, Pallas kernels, on_device(): pl.pallas_call(functools.partial(fix_kernel, boxes, slabs), out_shape=(pl...  1.09 us
    pallas_call x1, Pallas kernels, on_device(): pl.pallas_call(functools.partial(local_kernel, boxes, slabs, total_z), ou...  1 us
  transfers between devices with their start and end apart: 6, of which 4 were waited for; matrix products, arithmetic and copies ran while one was open for 0% of the time, Pallas kernels for 12%

commit v1 on v0

--- a/solution.py
+++ b/solution.py
@@ -14,6 +14,7 @@
 SMEM = pl.BlockSpec(memory_space=pltpu.SMEM)
 HBM = pl.BlockSpec(memory_space=pl.ANY)
 CORNERS = 8
+VALUE_FACES = 4
 PARAMS = pltpu.CompilerParams(vmem_limit_bytes=16 * 1024 * 1024)
 
 
@@ -76,7 +77,7 @@
 
 
 def pack_kernel(
-    slots, home, ids_in, weights_in, prof_in, now_in, prev_in, cour_in, cells_in, slabs,
+    slots, depth_devices, home, ids_in, weights_in, prof_in, now_in, prev_in, cour_in, cells_in, slabs,
     now, prev, cour, cells, planes, edges, za, zb, vals, xa, xb, ids, weights, prof, block, sems,
 ):
     _, members, width_x, width_z, _ = now.shape
@@ -85,10 +86,12 @@
     total_z = prof.shape[1]
     pairs = [(ids_in, ids), (prof_in, prof), (weights_in, weights)]
     for h in halves(now):
+        pairs.append((cour_in.at[:, :, pl.ds(h * LANES, LANES)], cour.at[h]))
+    groups = [len(pairs)]
+    for h in halves(now):
         pairs.append((now_in.at[:, :, :, pl.ds(h * LANES, LANES)], now.at[h]))
-    for h in halves(now):
-        pairs.append((cour_in.at[:, :, pl.ds(h * LANES, LANES)], cour.at[h]))
         pairs.append((prev_in.at[:, :, :, pl.ds(h * LANES, LANES)], prev.at[h]))
+    groups = groups + [len(pairs)] * members
     fields = len(pairs)
     pairs.append((slabs.at[lax.rem(home[0], slots)], block))
     pairs.append((cells_in, cells))
@@ -108,9 +111,7 @@
             beyond = 1.0 + prof[ids[m], jnp.clip(z, 0, total_z - 1)]
             edges[2 * m + s : 2 * m + s + 1] = jnp.full((1, LANES), beyond, F32)
     owner = slab == home[0] // slots
-    points = block.shape[1]
     width = vals.shape[1]
-    chunks = points // width
     sample = rows_of((samples, width), 0)
     columns = []
     for t in range(steps):
@@ -119,7 +120,7 @@
             column = jnp.where(sample == k, weights[t, k], column)
         columns.append(jnp.where(owner, column, 0.0))
     zero = jnp.zeros((1, LANES), F32)
-    for load in loads[3:fields]:
+    for load in loads[3 : groups[0]]:
         load.wait()
     face, side = lax.rem(box, 2), lax.rem(slab, 2)
 
@@ -131,52 +132,63 @@
             out.append(2.0 * here - prev_here + coef * (around - 6.0 * here))
         return out
 
-    for a, b, at_high, get, length in (
-        (za, zb, side == 0, "z", width_z),
-        (xa, xb, face == 0, "x", width_x),
-    ):
-        ends = []
-        for at, inner in ((0, 1), (length - 1, length - 2)):
-            parts = [[] for _ in halves(now)]
-            if get == "x":
-                courant = [cour[h, at] for h in halves(now)]
-            else:
-                courant = [depth_rows(cour, at, h) for h in halves(now)]
-            steps_here = []
-            for m in range(members):
-                if get == "x":
-                    heres, prevs, inners = (
-                        [ref[h, m, i] for h in halves(now)]
-                        for ref, i in ((now, at), (prev, at), (now, inner))
-                    )
-                    coefs = [c * planes[m] for c in courant]
-                else:
-                    heres, prevs, inners = (
-                        [depth_rows(ref, i, h, m) for h in halves(now)]
-                        for ref, i in ((now, at), (prev, at), (now, inner))
-                    )
-                    coefs = [c * (1.0 + prof[ids[m], start_z + at]) for c in courant]
-                steps_here.append(local_step(heres, prevs, inners, coefs))
-                for h in halves(now):
-                    parts[h].append(heres[h])
+    sides = (
+        (za, zb, side == 0, width_x, (0, 1), (width_z - 1, width_z - 2), True),
+        (xa, xb, face == 0, width_z, (0, 1), (width_x - 1, width_x - 2), False),
+    )
+
+    def plane(ref, at, deep, *lead):
+        return depth_rows(ref, at, *lead) if deep else ref[lead + (at,)]
+
+    def put(a, b, at_high, at, h, low, high):
+        n = low.shape[0]
+        a[at * n : (at + 1) * n, lanes(h)] = jnp.where(at_high, high, low)
+        b[at * n : (at + 1) * n, lanes(h)] = jnp.where(at_high, low, high)
+
+    for a, b, at_high, _, (low, _), (high, _), deep in sides:
+        for h in halves(now):
+            courant = [plane(cour, at, deep, h) for at in (low, high)]
+            put(a, b, at_high, 2 * members, h, *courant)
+    for m in range(members):
+        for load in loads[groups[m] : groups[m + 1]]:
+            load.wait()
+        for a, b, at_high, _, low, high, deep in sides:
+            ends = []
+            for at, inner in (low, high):
+                heres, prevs, inners = (
+                    [plane(ref, i, deep, h, m) for h in halves(now)]
+                    for ref, i in ((now, at), (prev, at), (now, inner))
+                )
+                scale = 1.0 + prof[ids[m], start_z + at] if deep else planes[m]
+                coefs = [plane(cour, at, deep, h) * scale for h in halves(now)]
+                ends.append((heres, local_step(heres, prevs, inners, coefs)))
             for h in halves(now):
-                ends.append(parts[h] + [r[h] for r in steps_here] + [courant[h]])
-        count = len(ends) // 2
-        for h in range(count):
-            for i, (low, high) in enumerate(zip(ends[h], ends[count + h])):
-                n = low.shape[0]
-                a[i * n : (i + 1) * n, lanes(h)] = jnp.where(at_high, high, low)
-                b[i * n : (i + 1) * n, lanes(h)] = jnp.where(at_high, low, high)
+                put(a, b, at_high, m, h, ends[0][0][h], ends[1][0][h])
+                put(a, b, at_high, members + m, h, ends[0][1][h], ends[1][1][h])
+    per_face = cells.shape[1]
+    per = per_face // width
+    low_half = slab < depth_devices // 2
+    tail = (2 * members + 1) * width_x
     loads[fields].wait()
-    for c in range(chunks):
-        piece = block[:, c * width : (c + 1) * width]
-        for t in range(steps):
-            at = t * chunks + c
-            vals[at : at + 1] = jnp.sum(columns[t] * piece, axis=0, keepdims=True)
+    picks = (
+        (0, jnp.where(box == 0, 0, 1), True, True),
+        (1, jnp.where(low_half, 2, 3), True, False),
+        (1, jnp.where(low_half, 3, 2), False, True),
+        (2, 4, True, True),
+        (3, 5, True, True),
+    )
+    for slot, f, for_near, for_far in picks:
+        for i in range(per):
+            start = pl.multiple_of(f * per_face + i * width, width)
+            piece = block[:, pl.ds(start, width)]
+            for t in range(steps):
+                at = (t * VALUE_FACES + slot) * per + i
+                row_value = jnp.sum(columns[t] * piece, axis=0, keepdims=True)
+                if for_near:
+                    vals[at : at + 1] = row_value
+                if for_far:
+                    zb[tail + at : tail + at + 1] = row_value
     loads[fields + 1].wait()
-    tail = (2 * members + 1) * width_x
-    offered = vals[...]
-    zb[tail:] = offered
 
 
 def relay_kernel(relay, face, vals, zb, after, za):
@@ -307,21 +319,20 @@
     steps = xsrc.shape[0]
     chunks = value.shape[0] // steps
     per = wide.shape[2] // depth_y
-    faces = faces_of(box, slab)
 
     def of_face(f):
         vs = []
         for t in range(steps):
-            pieces = [value[pl.ds(t * chunks + f * per + i, 1), :] for i in range(per)]
+            pieces = [value[t * chunks + f * per + i : t * chunks + f * per + i + 1, :] for i in range(per)]
             vs.append(jnp.concatenate(pieces, axis=1))
         return vs
 
-    for t, s in enumerate(face_source(of_face(faces[0]), rows_z[0], wide[0], width_z)):
+    for t, s in enumerate(face_source(of_face(0), rows_z[0], wide[0], width_z)):
         xsrc[t, : s.shape[0]] = s
-    for t, s in enumerate(face_source(of_face(faces[1]), rows_x[...], wide[1], width_x)):
+    for t, s in enumerate(face_source(of_face(1), rows_x[...], wide[1], width_x)):
         zsrc[t, : s.shape[0]] = s
     ys = [
-        face_source(of_face(faces[2 + i]), rows_z[1 + i], narrow[i], width_z) for i in range(2)
+        face_source(of_face(2 + i), rows_z[1 + i], narrow[i], width_z) for i in range(2)
     ]
 
     lane = rows_of((width_z, LANES), 1)
@@ -459,7 +470,7 @@
     slots, samples, points = stored_slabs.shape
     steps = interp_weights.shape[0]
     total_z = width_z * slabs
-    value_rows = steps * points // depth_y
+    value_rows = steps * VALUE_FACES * surface_cells.shape[1] // depth_y
     span_x = (2 * members + 1) * width_z
     span_z = (2 * members + 1) * width_x
     count = depth_y // LANES
@@ -491,7 +502,7 @@
     whole = pressure_now.shape
     half = (count,) + whole[:3] + (LANES,)
     now, prev, cour, cells, planes, edges, za, zb, vals, xa, xb = pl.pallas_call(
-        functools.partial(pack_kernel, slots),
+        functools.partial(pack_kernel, slots, slabs),
         out_shape=(
             inner(*half),
             inner(*half),
@@ -522,11 +533,12 @@
     )
 
     per_face = surface_cells.shape[1]
+    away = zb[span_z:]
     zb = over_slab(zb, pairs_odd(slabs))
     xa = over_box(xa, False)
     xb = over_box(xb, True)
     others = [
-        over_slab(vals, [i ^ k for i in range(slabs)])
+        over_slab(vals if k < slabs // 2 else away, [i ^ k for i in range(slabs)])
         for k in range(2, slabs)
         if slabs != 4
     ]

time: 20.2 us -> 19.8 us (0.980)
  waiting for transfers between devices: 9.26 us -> 8.98 us
    ppermute x4, waiting for transfers between devices: 5.66 us -> 5.37 us  [over_slab(): return lax.ppermute(x, 'slab', list(enumerate(partner)))]
where the time goes in v1:
time: 19.8 us; the launch traced here: 19.7 us
  waiting for transfers between devices  8.98 us (45%)
  Pallas kernels  5.23 us (26%)
  starting transfers between devices  4.14 us (21%)
  between operations  1.32 us (7%)
    ppermute x4, waiting for transfers between devices, over_slab(): return lax.ppermute(x, 'slab', list(enumerate(partner)))  5.37 us
    ppermute x2, waiting for transfers between devices, over_box(): return lax.ppermute(x, ('box', 'slab'), pairs)  3.6 us
    ppermute x4, starting transfers between devices, over_slab(): return lax.ppermute(x, 'slab', list(enumerate(partner)))  2.84 us
    pallas_call x1, Pallas kernels, on_device(): pl.pallas_call(functools.partial(pack_kernel, slots, slabs), out_shape=(i...  1.73 us
    pallas_call x1, Pallas kernels, on_device(): pl.pallas_call(functools.partial(main_kernel, boxes, slabs, len(others)),...  1.4 us
    ppermute x2, starting transfers between devices, over_box(): return lax.ppermute(x, ('box', 'slab'), pairs)  1.3 us
    pallas_call x1, Pallas kernels, on_device(): pl.pallas_call(functools.partial(fix_kernel, boxes, slabs), out_shape=(pl...  1.09 us
    pallas_call x1, Pallas kernels, on_device(): pl.pallas_call(functools.partial(local_kernel, boxes, slabs, total_z), ou...  1 us
  transfers between devices with their start and end apart: 6, of which 4 were waited for; matrix products, arithmetic and copies ran while one was open for 0% of the time, Pallas kernels for 12%

profile of v1, /device:TPU:19, one launch (start us, length us, event | category | flops | bytes accessed | tf_op | source)
XLA Modules:
  0.0 19.7 jit_solution(9390687965260543887)
XLA Ops:
  1.3 1.7 %pack.1 = (f32[2,2,16,16,128]{4,3,2,1,0:T(8,128)S(1)}, f32[2,2,16,16,128]{4,3,2,1,0:T(8,128)S(1)}, f32[2,16,16,128]{3,2,1,0:T(8,128)S(1)}, s32[6,1024]{1,0:T(8,1...) custom-call(s32[1]{0:T(128)S(6)} %copy.11.home, ...), custom_call_target="tpu_custom_call" | custom-call | tf_op jit(solution)/shard_map/pack/pallas_call | solution.py:504
  3.0 0.9 %collective-permute-start.2 = (f32[112,256]{1,0:T(8,128)S(1)}, f32[112,256]{1,0:T(8,128)S(1)}, u32[]{:S(2)}, u32[]{:S(2)}) collective-permute-start(f32[112,256]{1,0:T(8,128)S(1)} %get-tuple-element.27), channel_id=1, source_target_pairs={{0,3},{1,2},{2,1},{3,0},{4,7},{5,6},{6,5},{7,4},{8,11},{9,10},{10,... | collective-permute-start | bytes 344072 | tf_op jit(solution)/shard_map/ppermute | solution.py:488
  3.9 1.0 %local.1 = (f32[2,2,16,16,128]{4,3,2,1,0:T(8,128)S(1)}, bf16[2,256,1024]{2,1,0:T(8,128)(2,1)S(1)}, bf16[2,32,1024]{2,1,0:T(8,128)(2,1)S(1)}, bf16[32,1024]{1,0:T(8,128)(2,1)S(1)}, bf16[3,32,1024]{2,1,0:T(8,128)(2,1)S(1)}) custom-call(f32[2,16,128]{2,1,0:T(8,128)S(1)} %get-tuple-element.28.planes, s32[6,1024]{1,0:T(8,128)S(1)} %get-tuple-element.29.cells, ...), custom_call_target="tpu_custom_call" | custom-call | tf_op jit(solution)/shard_map/local/pallas_call | solution.py:550
  4.9 3.9 %collective-permute-done.2.zb = f32[112,256]{1,0:T(8,128)S(1)} collective-permute-done((f32[112,256]{1,0:T(8,128)S(1)}, f32[112,256]{1,0:T(8,128)S(1)}, u32[]{:S(2)}, u32[]{:S(2)}) %collective-permute-start.2) | collective-permute-done | bytes 114720 | tf_op jit(solution)/shard_map/ppermute | solution.py:488
  8.8 0.5 %collective-permute-start.5 = (f32[112,256]{1,0:T(8,128)S(1)}, f32[112,256]{1,0:T(8,128)S(1)}, u32[]{:S(2)}, u32[]{:S(2)}) collective-permute-start(f32[112,256]{1,0:T(8,128)S(1)} %relay.1.after), channel_id=1, source_target_pairs={{0,1},{1,0},{2,3},{3,2},{4,5},{5,4},{6,7},{7,6},{8,9},{9,8},{10,11... | collective-permute-start | bytes 344072 | tf_op jit(solution)/shard_map/ppermute | solution.py:488
  9.3 1.3 %collective-permute-start = (f32[80,256]{1,0:T(8,128)S(1)}, f32[80,256]{1,0:T(8,128)S(1)}, u32[]{:S(2)}, u32[]{:S(2)}) collective-permute-start(f32[80,256]{1,0:T(8,128)S(1)} %get-tuple-element.23), channel_id=1, source_target_pairs={{0,4},{1,5},{2,6},{3,7},{4,0},{5,1},{6,2},{7,3},{8,12},{9,13},{10,... | collective-permute-start | bytes 245768 | tf_op jit(solution)/shard_map/ppermute | solution.py:500
  10.6 0.0 collective-permute-start.1
  10.6 2.6 %collective-permute-done.xa = f32[80,256]{1,0:T(8,128)S(1)} collective-permute-done((f32[80,256]{1,0:T(8,128)S(1)}, f32[80,256]{1,0:T(8,128)S(1)}, u32[]{:S(2)}, u32[]{:S(2)}) %collective-permute-start) | collective-permute-done | bytes 81952 | tf_op jit(solution)/shard_map/ppermute | solution.py:500
  13.2 1.0 %collective-permute-done.1.xb = f32[80,256]{1,0:T(8,128)S(1)} collective-permute-done((f32[80,256]{1,0:T(8,128)S(1)}, f32[80,256]{1,0:T(8,128)S(1)}, u32[]{:S(2)}, u32[]{:S(2)}) %collective-permute-start.1) | collective-permute-done | bytes 81952 | tf_op jit(solution)/shard_map/ppermute | solution.py:500
  14.2 1.3 %collective-permute-start.3 = (f32[8,256]{1,0:T(8,128)S(1)}, f32[8,256]{1,0:T(8,128)S(1)}, u32[]{:S(2)}, u32[]{:S(2)}) collective-permute-start(f32[8,256]{1,0:T(8,128)S(1)} %get-tuple-element.34), channel_id=1, source_target_pairs={{0,1},{1,0},{2,3},{3,2},{4,5},{5,4},{6,7},{7,6},{8,9},{9,8},{10,11... | collective-permute-start | bytes 24584 | tf_op jit(solution)/shard_map/ppermute | solution.py:488
  15.5 0.2 collective-permute-start.4
  15.7 0.0 collective-permute-done.5.za
  15.7 1.4 %main.1 = (f32[2,2,16,16,128]{4,3,2,1,0:T(8,128)S(1)}, f32[2,2,16,16,128]{4,3,2,1,0:T(8,128)S(1)}, f32[8,256]{1,0:T(8,128)S(1)}) custom-call(f32[2,16,128]{2,1,0:T(8,128)S(1)} %get-tuple-element.28.planes, f32[4,128]{1,0:T(4,128)S(1)} %get-tuple-element.36.edges, bf16[2,256,1024]{2,1,0:T(8,128)(2,1)S(1)} %get-tuple-element.37.wide, ...), custom_call_target="tpu_custom_call" | custom-call | tf_op jit(solution)/shard_map/main/pallas_call | solution.py:587
  17.1 0.0 collective-permute-done.3.ca
  17.1 1.5 %collective-permute-done.4.cb = f32[8,256]{1,0:T(8,128)S(1)} collective-permute-done((f32[8,256]{1,0:T(8,128)S(1)}, f32[8,256]{1,0:T(8,128)S(1)}, u32[]{:S(2)}, u32[]{:S(2)}) %collective-permute-start.4) | collective-permute-done | bytes 8224 | tf_op jit(solution)/shard_map/ppermute | solution.py:488
  18.6 1.1 %fix.1 = (f32[2,16,16,256]{3,2,1,0:T(8,128)}, f32[2,16,16,256]{3,2,1,0:T(8,128)}) custom-call(f32[8,256]{1,0:T(8,128)S(1)} %collective-permute-done.3.ca, f32[8,256]{1,0:T(8,128)S(1)} %collective-permute-done.4.cb, f32[2,2,16,16,128]{4,3,2,1,0:T(8,128)S(1)} %get-tuple-element.41.one, f32[2,2,16,16,128]{4,3,2,1,0:T(8,128)S(1)} %get-tuple-element.42.nxt, ...), custom_call_target="tpu_custom_call" | custom-call | tf_op jit(solution)/shard_map/fix/pallas_call | solution.py:608
  (2 shorter events, 0.0 us)
Async XLA Ops:
  3.0 5.8 %collective-permute-start.2 = (f32[112,256]{1,0:T(8,128)S(1)}, f32[112,256]{1,0:T(8,128)S(1)}, u32[]{:S(2)}, u32[]{:S(2)}) collective-permute-start(f32[112,256]{1,0:T(8,128)S(1)} %get-tuple-element.27), channel_id=1, source_target_pairs={{0,3},{1,2},{2,1},{3,0},{4,7},{5,6},{6,5},{7,4},{8,11},{9,10},{10,... | collective-permute-start | bytes 344072 | tf_op jit(solution)/shard_map/ppermute | solution.py:488
  8.8 6.9 %collective-permute-start.5 = (f32[112,256]{1,0:T(8,128)S(1)}, f32[112,256]{1,0:T(8,128)S(1)}, u32[]{:S(2)}, u32[]{:S(2)}) collective-permute-start(f32[112,256]{1,0:T(8,128)S(1)} %relay.1.after), channel_id=1, source_target_pairs={{0,1},{1,0},{2,3},{3,2},{4,5},{5,4},{6,7},{7,6},{8,9},{9,8},{10,11... | collective-permute-start | bytes 344072 | tf_op jit(solution)/shard_map/ppermute | solution.py:488
  9.3 3.9 %collective-permute-start = (f32[80,256]{1,0:T(8,128)S(1)}, f32[80,256]{1,0:T(8,128)S(1)}, u32[]{:S(2)}, u32[]{:S(2)}) collective-permute-start(f32[80,256]{1,0:T(8,128)S(1)} %get-tuple-element.23), channel_id=1, source_target_pairs={{0,4},{1,5},{2,6},{3,7},{4,0},{5,1},{6,2},{7,3},{8,12},{9,13},{10,... | collective-permute-start | bytes 245768 | tf_op jit(solution)/shard_map/ppermute | solution.py:500
  10.6 3.6 %collective-permute-start.1 = (f32[80,256]{1,0:T(8,128)S(1)}, f32[80,256]{1,0:T(8,128)S(1)}, u32[]{:S(2)}, u32[]{:S(2)}) collective-permute-start(f32[80,256]{1,0:T(8,128)S(1)} %get-tuple-element.24), channel_id=1, source_target_pairs={{0,1},{1,0},{2,3},{3,2},{4,8},{5,9},{6,10},{7,11},{8,4},{9,5},{10,... | collective-permute-start | bytes 245768 | tf_op jit(solution)/shard_map/ppermute | solution.py:500
  14.2 2.9 %collective-permute-start.3 = (f32[8,256]{1,0:T(8,128)S(1)}, f32[8,256]{1,0:T(8,128)S(1)}, u32[]{:S(2)}, u32[]{:S(2)}) collective-permute-start(f32[8,256]{1,0:T(8,128)S(1)} %get-tuple-element.34), channel_id=1, source_target_pairs={{0,1},{1,0},{2,3},{3,2},{4,5},{5,4},{6,7},{7,6},{8,9},{9,8},{10,11... | collective-permute-start | bytes 24584 | tf_op jit(solution)/shard_map/ppermute | solution.py:488
  15.5 3.1 %collective-permute-start.4 = (f32[8,256]{1,0:T(8,128)S(1)}, f32[8,256]{1,0:T(8,128)S(1)}, u32[]{:S(2)}, u32[]{:S(2)}) collective-permute-start(f32[8,256]{1,0:T(8,128)S(1)} %get-tuple-element.35), channel_id=1, source_target_pairs={{0,3},{1,2},{2,1},{3,0},{4,7},{5,6},{6,5},{7,4},{8,11},{9,10},{10,... | collective-permute-start | bytes 24584 | tf_op jit(solution)/shard_map/ppermute | solution.py:488

commit v2 on v1

--- a/solution.py
+++ b/solution.py
@@ -298,7 +298,7 @@
     vals, za, zb, xa, xb, *rest,
 ):
     others, rest = rest[:received], rest[received:]
-    one, nxt, late, hz, xlo, xhi, zlo, zhi, value, xsrc, zsrc = rest
+    last, one, nxt, late, hz, xlo, xhi, zlo, zhi, value, xsrc, zsrc, sems = rest
     count, members, width_x, width_z, _ = now.shape
     depth_y = count * LANES
     box, slab = lax.axis_index("box"), lax.axis_index("slab")
@@ -386,9 +386,10 @@
                 base = ref[(members + m) * width_x : (members + m + 1) * width_x, lanes(h)]
                 hz[s, h, m] = base + coef * depth_rows(now, z, h, m) + source[h]
                 coef_z[s, m, h] = coef
-    for x in range(width_x):
-        source = plane_source(0, x)
-        for m in range(members):
+    sources = [plane_source(0, x) for x in range(width_x)]
+    copies = []
+    for m in range(members):
+        for x in range(width_x):
             at = m * width_x + x
             for h in range(count):
                 low_row, high_row = zlo[at : at + 1, lanes(h)], zhi[at : at + 1, lanes(h)]
@@ -397,7 +398,14 @@
                     more = more + xlo[m * width_z : (m + 1) * width_z, lanes(h)]
                 if x == width_x - 1:
                     more = more + xhi[m * width_z : (m + 1) * width_z, lanes(h)]
-                one[h, m, x] = local[h, m, x] + (cour[h, x] * planes[m]) * more + source[h]
+                one[h, m, x] = local[h, m, x] + (cour[h, x] * planes[m]) * more + sources[x][h]
+        for h in range(count):
+            copies.append(
+                pltpu.make_async_copy(
+                    one.at[h, m], last.at[m, :, :, pl.ds(h * LANES, LANES)], sems.at[len(copies)]
+                )
+            )
+            copies[-1].start()
     for x in range(width_x):
         source = plane_source(1, x)
         for m in range(members):
@@ -416,9 +424,11 @@
                         beyond = coef_z[e, m, h][x : x + 1] + coef_x[s, m, h][z : z + 1]
                         at = 2 * (members * e + m) + s
                         late[at : at + 1, lanes(h)] = coef[z : z + 1] * beyond
-
-
-def fix_kernel(boxes, slabs, ca, cb, one, nxt, late, out, last, done, sems):
+    for copy in copies:
+        copy.wait()
+
+
+def fix_kernel(boxes, slabs, ca, cb, one, nxt, late, first, out, last, done, sems):
     count, members, width_x, width_z, _ = nxt.shape
     box, slab = lax.axis_index("box"), lax.axis_index("slab")
     side = lax.rem(slab, 2)
@@ -435,7 +445,6 @@
         inside = pl.ds(1, width_x - 2)
         for m in range(members):
             send(nxt.at[h, m, inside], out.at[m, inside, :, pl.ds(h * LANES, LANES)])
-            send(one.at[h, m], last.at[m, :, :, pl.ds(h * LANES, LANES)])
     for h in range(count):
         for m in range(members):
             for s, x in ((0, 0), (1, width_x - 1)):
@@ -584,11 +593,13 @@
     cb = over_slab(cb, pairs_odd(slabs))
     za, ca, cb = near(za, ca, cb)
 
-    one, nxt, late = pl.pallas_call(
+    last, one, nxt, late = pl.pallas_call(
         functools.partial(main_kernel, boxes, slabs, len(others)),
-        out_shape=(inner(*half), inner(*half), inner(4 * members, depth_y)),
+        out_shape=(
+            pltpu.HBM(whole, F32), inner(*half), inner(*half), inner(4 * members, depth_y),
+        ),
         in_specs=[VMEM] * (14 + len(others)),
-        out_specs=(VMEM, VMEM, VMEM),
+        out_specs=(HBM, VMEM, VMEM, VMEM),
         scratch_shapes=[
             inner(2, count, members, width_x, LANES),
             inner(span_x, depth_y),
@@ -598,6 +609,7 @@
             inner(value_rows, depth_y),
             inner(steps, high_z, depth_y),
             inner(steps, high_x, depth_y),
+            pltpu.SemaphoreType.DMA((count * members,)),
         ],
         compiler_params=PARAMS,
         name="main",
@@ -608,15 +620,16 @@
     return pl.pallas_call(
         functools.partial(fix_kernel, boxes, slabs),
         out_shape=(pltpu.HBM(whole, F32),) * 2,
-        in_specs=[VMEM] * 5,
+        in_specs=[VMEM] * 5 + [HBM],
         out_specs=(HBM, HBM),
+        input_output_aliases={5: 1},
         scratch_shapes=[
             inner(count, 2, members, width_z, LANES),
             pltpu.SemaphoreType.DMA((4 * count * members,)),
         ],
         compiler_params=PARAMS,
         name="fix",
-    )(ca, cb, *near(one, nxt, late))
+    )(ca, cb, *near(one, nxt, late), *far(last))
 
 
 def solution(mesh):

time: 19.8 us -> 19.7 us (level)
  waiting for transfers between devices: 8.98 us -> 8.62 us
    ppermute x4, waiting for transfers between devices: 5.37 us -> 5.01 us  [over_slab(): return lax.ppermute(x, 'slab', list(enumerate(partner)))]
    pallas_call x1, Pallas kernels: 1.4 us -> 1.75 us  [on_device(): pl.pallas_call(functools.partial(main_kernel, boxes, slabs, len(others)),...]
  transfers between devices with their start and end apart: 6 -> 6, of which waited for: 4 -> 4; matrix products, arithmetic and copies ran while one was open for 0% -> 0% of each run, Pallas kernels for 12% -> 14%
where the time goes in v2:
time: 19.7 us; the launch traced here: 19.5 us
  waiting for transfers between devices  8.62 us (44%)
  Pallas kernels  5.42 us (28%)
  starting transfers between devices  4.14 us (21%)
  between operations  1.32 us (7%)
    ppermute x4, waiting for transfers between devices, over_slab(): return lax.ppermute(x, 'slab', list(enumerate(partner)))  5.01 us
    ppermute x2, waiting for transfers between devices, over_box(): return lax.ppermute(x, ('box', 'slab'), pairs)  3.6 us
    ppermute x4, starting transfers between devices, over_slab(): return lax.ppermute(x, 'slab', list(enumerate(partner)))  2.84 us
    pallas_call x1, Pallas kernels, on_device(): pl.pallas_call(functools.partial(main_kernel, boxes, slabs, len(others)),...  1.75 us
    pallas_call x1, Pallas kernels, on_device(): pl.pallas_call(functools.partial(pack_kernel, slots, slabs), out_shape=(i...  1.73 us
    ppermute x2, starting transfers between devices, over_box(): return lax.ppermute(x, ('box', 'slab'), pairs)  1.3 us
    pallas_call x1, Pallas kernels, on_device(): pl.pallas_call(functools.partial(local_kernel, boxes, slabs, total_z), ou...  1 us
    pallas_call x1, Pallas kernels, on_device(): pl.pallas_call(functools.partial(fix_kernel, boxes, slabs), out_shape=(pl...  0.92 us
  transfers between devices with their start and end apart: 6, of which 4 were waited for; matrix products, arithmetic and copies ran while one was open for 0% of the time, Pallas kernels for 14%

profile of v2, /device:TPU:19, one launch (start us, length us, event | category | flops | bytes accessed | tf_op | source)
XLA Modules:
  0.0 19.5 jit_solution(15489743590405226317)
XLA Ops:
  1.3 1.7 %pack.1 = (f32[2,2,16,16,128]{4,3,2,1,0:T(8,128)S(1)}, f32[2,2,16,16,128]{4,3,2,1,0:T(8,128)S(1)}, f32[2,16,16,128]{3,2,1,0:T(8,128)S(1)}, s32[6,1024]{1,0:T(8,1...) custom-call(s32[1]{0:T(128)S(6)} %copy.13.home, ...), custom_call_target="tpu_custom_call" | custom-call | tf_op jit(solution)/shard_map/pack/pallas_call | solution.py:513
  3.0 0.9 %collective-permute-start.2 = (f32[112,256]{1,0:T(8,128)S(1)}, f32[112,256]{1,0:T(8,128)S(1)}, u32[]{:S(2)}, u32[]{:S(2)}) collective-permute-start(f32[112,256]{1,0:T(8,128)S(1)} %get-tuple-element.28), channel_id=1, source_target_pairs={{0,3},{1,2},{2,1},{3,0},{4,7},{5,6},{6,5},{7,4},{8,11},{9,10},{10,... | collective-permute-start | bytes 344072 | tf_op jit(solution)/shard_map/ppermute | solution.py:497
  3.9 1.0 %local.1 = (f32[2,2,16,16,128]{4,3,2,1,0:T(8,128)S(1)}, bf16[2,256,1024]{2,1,0:T(8,128)(2,1)S(1)}, bf16[2,32,1024]{2,1,0:T(8,128)(2,1)S(1)}, bf16[32,1024]{1,0:T(8,128)(2,1)S(1)}, bf16[3,32,1024]{2,1,0:T(8,128)(2,1)S(1)}) custom-call(f32[2,16,128]{2,1,0:T(8,128)S(1)} %get-tuple-element.29.planes, s32[6,1024]{1,0:T(8,128)S(1)} %get-tuple-element.30.cells, ...), custom_call_target="tpu_custom_call" | custom-call | tf_op jit(solution)/shard_map/local/pallas_call | solution.py:559
  4.9 3.9 %collective-permute-done.2.zb = f32[112,256]{1,0:T(8,128)S(1)} collective-permute-done((f32[112,256]{1,0:T(8,128)S(1)}, f32[112,256]{1,0:T(8,128)S(1)}, u32[]{:S(2)}, u32[]{:S(2)}) %collective-permute-start.2) | collective-permute-done | bytes 114720 | tf_op jit(solution)/shard_map/ppermute | solution.py:497
  8.8 0.5 %collective-permute-start.5 = (f32[112,256]{1,0:T(8,128)S(1)}, f32[112,256]{1,0:T(8,128)S(1)}, u32[]{:S(2)}, u32[]{:S(2)}) collective-permute-start(f32[112,256]{1,0:T(8,128)S(1)} %relay.1.after), channel_id=1, source_target_pairs={{0,1},{1,0},{2,3},{3,2},{4,5},{5,4},{6,7},{7,6},{8,9},{9,8},{10,11... | collective-permute-start | bytes 344072 | tf_op jit(solution)/shard_map/ppermute | solution.py:497
  9.3 1.3 %collective-permute-start = (f32[80,256]{1,0:T(8,128)S(1)}, f32[80,256]{1,0:T(8,128)S(1)}, u32[]{:S(2)}, u32[]{:S(2)}) collective-permute-start(f32[80,256]{1,0:T(8,128)S(1)} %get-tuple-element.24), channel_id=1, source_target_pairs={{0,4},{1,5},{2,6},{3,7},{4,0},{5,1},{6,2},{7,3},{8,12},{9,13},{10,... | collective-permute-start | bytes 245768 | tf_op jit(solution)/shard_map/ppermute | solution.py:509
  10.6 0.0 collective-permute-start.1
  10.6 2.6 %collective-permute-done.xa = f32[80,256]{1,0:T(8,128)S(1)} collective-permute-done((f32[80,256]{1,0:T(8,128)S(1)}, f32[80,256]{1,0:T(8,128)S(1)}, u32[]{:S(2)}, u32[]{:S(2)}) %collective-permute-start) | collective-permute-done | bytes 81952 | tf_op jit(solution)/shard_map/ppermute | solution.py:509
  13.2 1.0 %collective-permute-done.1.xb = f32[80,256]{1,0:T(8,128)S(1)} collective-permute-done((f32[80,256]{1,0:T(8,128)S(1)}, f32[80,256]{1,0:T(8,128)S(1)}, u32[]{:S(2)}, u32[]{:S(2)}) %collective-permute-start.1) | collective-permute-done | bytes 81952 | tf_op jit(solution)/shard_map/ppermute | solution.py:509
  14.2 1.3 %collective-permute-start.3 = (f32[8,256]{1,0:T(8,128)S(1)}, f32[8,256]{1,0:T(8,128)S(1)}, u32[]{:S(2)}, u32[]{:S(2)}) collective-permute-start(f32[8,256]{1,0:T(8,128)S(1)} %get-tuple-element.35), channel_id=1, source_target_pairs={{0,1},{1,0},{2,3},{3,2},{4,5},{5,4},{6,7},{7,6},{8,9},{9,8},{10,11... | collective-permute-start | bytes 24584 | tf_op jit(solution)/shard_map/ppermute | solution.py:497
  15.5 0.2 collective-permute-start.4
  15.7 0.0 collective-permute-done.5.za
  15.7 1.8 %main.1 = (f32[2,16,16,256]{3,2,1,0:T(8,128)}, f32[2,2,16,16,128]{4,3,2,1,0:T(8,128)S(1)}, f32[2,2,16,16,128]{4,3,2,1,0:T(8,128)S(1)}, f32[8,256]{1,0:T(8,128)S(1)}) custom-call(f32[2,16,128]{2,1,0:T(8,128)S(1)} %get-tuple-element.29.planes, f32[4,128]{1,0:T(4,128)S(1)} %get-tuple-element.37.edges, bf16[2,256,1024]{2,1,0:T(8,128)(2,1)S(1)} %get-tuple-element.38.wide, ...), custom_call_target="tpu_custom_call" | custom-call | tf_op jit(solution)/shard_map/main/pallas_call | solution.py:596
  17.5 0.0 collective-permute-done.3.ca
  17.5 1.1 %collective-permute-done.4.cb = f32[8,256]{1,0:T(8,128)S(1)} collective-permute-done((f32[8,256]{1,0:T(8,128)S(1)}, f32[8,256]{1,0:T(8,128)S(1)}, u32[]{:S(2)}, u32[]{:S(2)}) %collective-permute-start.4) | collective-permute-done | bytes 8224 | tf_op jit(solution)/shard_map/ppermute | solution.py:497
  18.6 0.9 %fix.1 = (f32[2,16,16,256]{3,2,1,0:T(8,128)}, f32[2,16,16,256]{3,2,1,0:T(8,128)}) custom-call(f32[8,256]{1,0:T(8,128)S(1)} %collective-permute-done.3.ca, f32[8,256]{1,0:T(8,128)S(1)} %collective-permute-done.4.cb, f32[2,2,16,16,128]{4,3,2,1,0:T(8,128)S(1)} %get-tuple-element.42.one, ...), custom_call_target="tpu_custom_call", output_to_operand_aliasing={{1}: (5, {})} | custom-call | tf_op jit(solution)/shard_map/fix/pallas_call | solution.py:620
  (2 shorter events, 0.0 us)
Async XLA Ops:
  3.0 5.8 %collective-permute-start.2 = (f32[112,256]{1,0:T(8,128)S(1)}, f32[112,256]{1,0:T(8,128)S(1)}, u32[]{:S(2)}, u32[]{:S(2)}) collective-permute-start(f32[112,256]{1,0:T(8,128)S(1)} %get-tuple-element.28), channel_id=1, source_target_pairs={{0,3},{1,2},{2,1},{3,0},{4,7},{5,6},{6,5},{7,4},{8,11},{9,10},{10,... | collective-permute-start | bytes 344072 | tf_op jit(solution)/shard_map/ppermute | solution.py:497
  8.8 6.9 %collective-permute-start.5 = (f32[112,256]{1,0:T(8,128)S(1)}, f32[112,256]{1,0:T(8,128)S(1)}, u32[]{:S(2)}, u32[]{:S(2)}) collective-permute-start(f32[112,256]{1,0:T(8,128)S(1)} %relay.1.after), channel_id=1, source_target_pairs={{0,1},{1,0},{2,3},{3,2},{4,5},{5,4},{6,7},{7,6},{8,9},{9,8},{10,11... | collective-permute-start | bytes 344072 | tf_op jit(solution)/shard_map/ppermute | solution.py:497
  9.3 3.9 %collective-permute-start = (f32[80,256]{1,0:T(8,128)S(1)}, f32[80,256]{1,0:T(8,128)S(1)}, u32[]{:S(2)}, u32[]{:S(2)}) collective-permute-start(f32[80,256]{1,0:T(8,128)S(1)} %get-tuple-element.24), channel_id=1, source_target_pairs={{0,4},{1,5},{2,6},{3,7},{4,0},{5,1},{6,2},{7,3},{8,12},{9,13},{10,... | collective-permute-start | bytes 245768 | tf_op jit(solution)/shard_map/ppermute | solution.py:509
  10.6 3.6 %collective-permute-start.1 = (f32[80,256]{1,0:T(8,128)S(1)}, f32[80,256]{1,0:T(8,128)S(1)}, u32[]{:S(2)}, u32[]{:S(2)}) collective-permute-start(f32[80,256]{1,0:T(8,128)S(1)} %get-tuple-element.25), channel_id=1, source_target_pairs={{0,1},{1,0},{2,3},{3,2},{4,8},{5,9},{6,10},{7,11},{8,4},{9,5},{10,... | collective-permute-start | bytes 245768 | tf_op jit(solution)/shard_map/ppermute | solution.py:509
  14.2 3.3 %collective-permute-start.3 = (f32[8,256]{1,0:T(8,128)S(1)}, f32[8,256]{1,0:T(8,128)S(1)}, u32[]{:S(2)}, u32[]{:S(2)}) collective-permute-start(f32[8,256]{1,0:T(8,128)S(1)} %get-tuple-element.35), channel_id=1, source_target_pairs={{0,1},{1,0},{2,3},{3,2},{4,5},{5,4},{6,7},{7,6},{8,9},{9,8},{10,11... | collective-permute-start | bytes 24584 | tf_op jit(solution)/shard_map/ppermute | solution.py:497
  15.5 3.1 %collective-permute-start.4 = (f32[8,256]{1,0:T(8,128)S(1)}, f32[8,256]{1,0:T(8,128)S(1)}, u32[]{:S(2)}, u32[]{:S(2)}) collective-permute-start(f32[8,256]{1,0:T(8,128)S(1)} %get-tuple-element.36), channel_id=1, source_target_pairs={{0,3},{1,2},{2,1},{3,0},{4,7},{5,6},{6,5},{7,4},{8,11},{9,10},{10,... | collective-permute-start | bytes 24584 | tf_op jit(solution)/shard_map/ppermute | solution.py:497

commit v3 on v2

--- a/solution.py
+++ b/solution.py
@@ -443,11 +443,10 @@
 
     for h in range(count):
         inside = pl.ds(1, width_x - 2)
-        for m in range(members):
-            send(nxt.at[h, m, inside], out.at[m, inside, :, pl.ds(h * LANES, LANES)])
+        send(nxt.at[h, :, inside], out.at[:, inside, :, pl.ds(h * LANES, LANES)])
     for h in range(count):
-        for m in range(members):
-            for s, x in ((0, 0), (1, width_x - 1)):
+        for s, x in ((0, 0), (1, width_x - 1)):
+            for m in range(members):
                 at = 2 * m + s
                 add = 0.0
                 for e, z in ((0, 0), (1, width_z - 1)):
@@ -458,7 +457,7 @@
                     k = 2 * members * e + at
                     add = jnp.where(row == z, late[k : k + 1, lanes(h)] * got, add)
                 done[h, s, m] = nxt[h, m, x] + add
-                send(done.at[h, s, m], out.at[m, x, :, pl.ds(h * LANES, LANES)])
+            send(done.at[h, s], out.at[:, x, :, pl.ds(h * LANES, LANES)])
     for copy in copies:
         copy.wait()
 
@@ -625,7 +624,7 @@
         input_output_aliases={5: 1},
         scratch_shapes=[
             inner(count, 2, members, width_z, LANES),
-            pltpu.SemaphoreType.DMA((4 * count * members,)),
+            pltpu.SemaphoreType.DMA((3 * count,)),
         ],
         compiler_params=PARAMS,
         name="fix",

time: 19.7 us -> 19.6 us (level)
  no operation moved by 1% of the time
where the time goes in v3:
time: 19.6 us; the launch traced here: 19.4 us
  waiting for transfers between devices  8.62 us (44%)
  Pallas kernels  5.33 us (27%)
  starting transfers between devices  4.14 us (21%)
  between operations  1.32 us (7%)
    ppermute x4, waiting for transfers between devices, over_slab(): return lax.ppermute(x, 'slab', list(enumerate(partner)))  5.01 us
    ppermute x2, waiting for transfers between devices, over_box(): return lax.ppermute(x, ('box', 'slab'), pairs)  3.6 us
    ppermute x4, starting transfers between devices, over_slab(): return lax.ppermute(x, 'slab', list(enumerate(partner)))  2.84 us
    pallas_call x1, Pallas kernels, on_device(): pl.pallas_call(functools.partial(main_kernel, boxes, slabs, len(others)),...  1.75 us
    pallas_call x1, Pallas kernels, on_device(): pl.pallas_call(functools.partial(pack_kernel, slots, slabs), out_shape=(i...  1.73 us
    ppermute x2, starting transfers between devices, over_box(): return lax.ppermute(x, ('box', 'slab'), pairs)  1.3 us
    pallas_call x1, Pallas kernels, on_device(): pl.pallas_call(functools.partial(local_kernel, boxes, slabs, total_z), ou...  1 us
    pallas_call x1, Pallas kernels, on_device(): pl.pallas_call(functools.partial(fix_kernel, boxes, slabs), out_shape=(pl...  0.83 us
  transfers between devices with their start and end apart: 6, of which 4 were waited for; matrix products, arithmetic and copies ran while one was open for 0% of the time, Pallas kernels for 14%

profile of v3, /device:TPU:19, one launch (start us, length us, event | category | flops | bytes accessed | tf_op | source)
XLA Modules:
  0.0 19.4 jit_solution(16059448150492606014)
XLA Ops:
  1.3 1.7 %pack.1 = (f32[2,2,16,16,128]{4,3,2,1,0:T(8,128)S(1)}, f32[2,2,16,16,128]{4,3,2,1,0:T(8,128)S(1)}, f32[2,16,16,128]{3,2,1,0:T(8,128)S(1)}, s32[6,1024]{1,0:T(8,1...) custom-call(s32[1]{0:T(128)S(6)} %copy.13.home, ...), custom_call_target="tpu_custom_call" | custom-call | tf_op jit(solution)/shard_map/pack/pallas_call | solution.py:512
  3.0 0.9 %collective-permute-start.2 = (f32[112,256]{1,0:T(8,128)S(1)}, f32[112,256]{1,0:T(8,128)S(1)}, u32[]{:S(2)}, u32[]{:S(2)}) collective-permute-start(f32[112,256]{1,0:T(8,128)S(1)} %get-tuple-element.28), channel_id=1, source_target_pairs={{0,3},{1,2},{2,1},{3,0},{4,7},{5,6},{6,5},{7,4},{8,11},{9,10},{10,... | collective-permute-start | bytes 344072 | tf_op jit(solution)/shard_map/ppermute | solution.py:496
  3.9 1.0 %local.1 = (f32[2,2,16,16,128]{4,3,2,1,0:T(8,128)S(1)}, bf16[2,256,1024]{2,1,0:T(8,128)(2,1)S(1)}, bf16[2,32,1024]{2,1,0:T(8,128)(2,1)S(1)}, bf16[32,1024]{1,0:T(8,128)(2,1)S(1)}, bf16[3,32,1024]{2,1,0:T(8,128)(2,1)S(1)}) custom-call(f32[2,16,128]{2,1,0:T(8,128)S(1)} %get-tuple-element.29.planes, s32[6,1024]{1,0:T(8,128)S(1)} %get-tuple-element.30.cells, ...), custom_call_target="tpu_custom_call" | custom-call | tf_op jit(solution)/shard_map/local/pallas_call | solution.py:558
  4.9 3.9 %collective-permute-done.2.zb = f32[112,256]{1,0:T(8,128)S(1)} collective-permute-done((f32[112,256]{1,0:T(8,128)S(1)}, f32[112,256]{1,0:T(8,128)S(1)}, u32[]{:S(2)}, u32[]{:S(2)}) %collective-permute-start.2) | collective-permute-done | bytes 114720 | tf_op jit(solution)/shard_map/ppermute | solution.py:496
  8.8 0.5 %collective-permute-start.5 = (f32[112,256]{1,0:T(8,128)S(1)}, f32[112,256]{1,0:T(8,128)S(1)}, u32[]{:S(2)}, u32[]{:S(2)}) collective-permute-start(f32[112,256]{1,0:T(8,128)S(1)} %relay.1.after), channel_id=1, source_target_pairs={{0,1},{1,0},{2,3},{3,2},{4,5},{5,4},{6,7},{7,6},{8,9},{9,8},{10,11... | collective-permute-start | bytes 344072 | tf_op jit(solution)/shard_map/ppermute | solution.py:496
  9.3 1.3 %collective-permute-start = (f32[80,256]{1,0:T(8,128)S(1)}, f32[80,256]{1,0:T(8,128)S(1)}, u32[]{:S(2)}, u32[]{:S(2)}) collective-permute-start(f32[80,256]{1,0:T(8,128)S(1)} %get-tuple-element.24), channel_id=1, source_target_pairs={{0,4},{1,5},{2,6},{3,7},{4,0},{5,1},{6,2},{7,3},{8,12},{9,13},{10,... | collective-permute-start | bytes 245768 | tf_op jit(solution)/shard_map/ppermute | solution.py:508
  10.6 0.0 collective-permute-start.1
  10.6 2.6 %collective-permute-done.xa = f32[80,256]{1,0:T(8,128)S(1)} collective-permute-done((f32[80,256]{1,0:T(8,128)S(1)}, f32[80,256]{1,0:T(8,128)S(1)}, u32[]{:S(2)}, u32[]{:S(2)}) %collective-permute-start) | collective-permute-done | bytes 81952 | tf_op jit(solution)/shard_map/ppermute | solution.py:508
  13.2 1.0 %collective-permute-done.1.xb = f32[80,256]{1,0:T(8,128)S(1)} collective-permute-done((f32[80,256]{1,0:T(8,128)S(1)}, f32[80,256]{1,0:T(8,128)S(1)}, u32[]{:S(2)}, u32[]{:S(2)}) %collective-permute-start.1) | collective-permute-done | bytes 81952 | tf_op jit(solution)/shard_map/ppermute | solution.py:508
  14.2 1.3 %collective-permute-start.3 = (f32[8,256]{1,0:T(8,128)S(1)}, f32[8,256]{1,0:T(8,128)S(1)}, u32[]{:S(2)}, u32[]{:S(2)}) collective-permute-start(f32[8,256]{1,0:T(8,128)S(1)} %get-tuple-element.35), channel_id=1, source_target_pairs={{0,1},{1,0},{2,3},{3,2},{4,5},{5,4},{6,7},{7,6},{8,9},{9,8},{10,11... | collective-permute-start | bytes 24584 | tf_op jit(solution)/shard_map/ppermute | solution.py:496
  15.5 0.2 collective-permute-start.4
  15.7 0.0 collective-permute-done.5.za
  15.7 1.8 %main.1 = (f32[2,16,16,256]{3,2,1,0:T(8,128)}, f32[2,2,16,16,128]{4,3,2,1,0:T(8,128)S(1)}, f32[2,2,16,16,128]{4,3,2,1,0:T(8,128)S(1)}, f32[8,256]{1,0:T(8,128)S(1)}) custom-call(f32[2,16,128]{2,1,0:T(8,128)S(1)} %get-tuple-element.29.planes, f32[4,128]{1,0:T(4,128)S(1)} %get-tuple-element.37.edges, bf16[2,256,1024]{2,1,0:T(8,128)(2,1)S(1)} %get-tuple-element.38.wide, ...), custom_call_target="tpu_custom_call" | custom-call | tf_op jit(solution)/shard_map/main/pallas_call | solution.py:595
  17.5 0.0 collective-permute-done.3.ca
  17.5 1.1 %collective-permute-done.4.cb = f32[8,256]{1,0:T(8,128)S(1)} collective-permute-done((f32[8,256]{1,0:T(8,128)S(1)}, f32[8,256]{1,0:T(8,128)S(1)}, u32[]{:S(2)}, u32[]{:S(2)}) %collective-permute-start.4) | collective-permute-done | bytes 8224 | tf_op jit(solution)/shard_map/ppermute | solution.py:496
  18.6 0.8 %fix.1 = (f32[2,16,16,256]{3,2,1,0:T(8,128)}, f32[2,16,16,256]{3,2,1,0:T(8,128)}) custom-call(f32[8,256]{1,0:T(8,128)S(1)} %collective-permute-done.3.ca, f32[8,256]{1,0:T(8,128)S(1)} %collective-permute-done.4.cb, f32[2,2,16,16,128]{4,3,2,1,0:T(8,128)S(1)} %get-tuple-element.42.one, ...), custom_call_target="tpu_custom_call", output_to_operand_aliasing={{1}: (5, {})} | custom-call | tf_op jit(solution)/shard_map/fix/pallas_call | solution.py:619
  (2 shorter events, 0.0 us)
Async XLA Ops:
  3.0 5.8 %collective-permute-start.2 = (f32[112,256]{1,0:T(8,128)S(1)}, f32[112,256]{1,0:T(8,128)S(1)}, u32[]{:S(2)}, u32[]{:S(2)}) collective-permute-start(f32[112,256]{1,0:T(8,128)S(1)} %get-tuple-element.28), channel_id=1, source_target_pairs={{0,3},{1,2},{2,1},{3,0},{4,7},{5,6},{6,5},{7,4},{8,11},{9,10},{10,... | collective-permute-start | bytes 344072 | tf_op jit(solution)/shard_map/ppermute | solution.py:496
  8.8 6.9 %collective-permute-start.5 = (f32[112,256]{1,0:T(8,128)S(1)}, f32[112,256]{1,0:T(8,128)S(1)}, u32[]{:S(2)}, u32[]{:S(2)}) collective-permute-start(f32[112,256]{1,0:T(8,128)S(1)} %relay.1.after), channel_id=1, source_target_pairs={{0,1},{1,0},{2,3},{3,2},{4,5},{5,4},{6,7},{7,6},{8,9},{9,8},{10,11... | collective-permute-start | bytes 344072 | tf_op jit(solution)/shard_map/ppermute | solution.py:496
  9.3 3.9 %collective-permute-start = (f32[80,256]{1,0:T(8,128)S(1)}, f32[80,256]{1,0:T(8,128)S(1)}, u32[]{:S(2)}, u32[]{:S(2)}) collective-permute-start(f32[80,256]{1,0:T(8,128)S(1)} %get-tuple-element.24), channel_id=1, source_target_pairs={{0,4},{1,5},{2,6},{3,7},{4,0},{5,1},{6,2},{7,3},{8,12},{9,13},{10,... | collective-permute-start | bytes 245768 | tf_op jit(solution)/shard_map/ppermute | solution.py:508
  10.6 3.6 %collective-permute-start.1 = (f32[80,256]{1,0:T(8,128)S(1)}, f32[80,256]{1,0:T(8,128)S(1)}, u32[]{:S(2)}, u32[]{:S(2)}) collective-permute-start(f32[80,256]{1,0:T(8,128)S(1)} %get-tuple-element.25), channel_id=1, source_target_pairs={{0,1},{1,0},{2,3},{3,2},{4,8},{5,9},{6,10},{7,11},{8,4},{9,5},{10,... | collective-permute-start | bytes 245768 | tf_op jit(solution)/shard_map/ppermute | solution.py:508
  14.2 3.3 %collective-permute-start.3 = (f32[8,256]{1,0:T(8,128)S(1)}, f32[8,256]{1,0:T(8,128)S(1)}, u32[]{:S(2)}, u32[]{:S(2)}) collective-permute-start(f32[8,256]{1,0:T(8,128)S(1)} %get-tuple-element.35), channel_id=1, source_target_pairs={{0,1},{1,0},{2,3},{3,2},{4,5},{5,4},{6,7},{7,6},{8,9},{9,8},{10,11... | collective-permute-start | bytes 24584 | tf_op jit(solution)/shard_map/ppermute | solution.py:496
  15.5 3.1 %collective-permute-start.4 = (f32[8,256]{1,0:T(8,128)S(1)}, f32[8,256]{1,0:T(8,128)S(1)}, u32[]{:S(2)}, u32[]{:S(2)}) collective-permute-start(f32[8,256]{1,0:T(8,128)S(1)} %get-tuple-element.36), channel_id=1, source_target_pairs={{0,3},{1,2},{2,1},{3,0},{4,7},{5,6},{6,5},{7,4},{8,11},{9,10},{10,... | collective-permute-start | bytes 24584 | tf_op jit(solution)/shard_map/ppermute | solution.py:496

commit v4 on v3

--- a/solution.py
+++ b/solution.py
@@ -96,8 +96,15 @@
     pairs.append((slabs.at[lax.rem(home[0], slots)], block))
     pairs.append((cells_in, cells))
     loads = [pltpu.make_async_copy(a, b, sems.at[i]) for i, (a, b) in enumerate(pairs)]
-    for load in loads:
+    owner = slab == home[0] // slots
+    for load in loads[:fields]:
         load.start()
+
+    @pl.when(owner)
+    def _():
+        loads[fields].start()
+
+    loads[fields + 1].start()
     start_z = slab * width_z
     for load in loads[:3]:
         load.wait()
@@ -110,7 +117,6 @@
         for s, z in ((0, start_z - 1), (1, start_z + width_z)):
             beyond = 1.0 + prof[ids[m], jnp.clip(z, 0, total_z - 1)]
             edges[2 * m + s : 2 * m + s + 1] = jnp.full((1, LANES), beyond, F32)
-    owner = slab == home[0] // slots
     width = vals.shape[1]
     sample = rows_of((samples, width), 0)
     columns = []
@@ -118,7 +124,7 @@
         column = jnp.zeros((samples, width), F32)
         for k in range(samples):
             column = jnp.where(sample == k, weights[t, k], column)
-        columns.append(jnp.where(owner, column, 0.0))
+        columns.append(column)
     zero = jnp.zeros((1, LANES), F32)
     for load in loads[3 : groups[0]]:
         load.wait()
@@ -169,7 +175,6 @@
     per = per_face // width
     low_half = slab < depth_devices // 2
     tail = (2 * members + 1) * width_x
-    loads[fields].wait()
     picks = (
         (0, jnp.where(box == 0, 0, 1), True, True),
         (1, jnp.where(low_half, 2, 3), True, False),
@@ -177,17 +182,27 @@
         (2, 4, True, True),
         (3, 5, True, True),
     )
-    for slot, f, for_near, for_far in picks:
-        for i in range(per):
-            start = pl.multiple_of(f * per_face + i * width, width)
-            piece = block[:, pl.ds(start, width)]
-            for t in range(steps):
-                at = (t * VALUE_FACES + slot) * per + i
-                row_value = jnp.sum(columns[t] * piece, axis=0, keepdims=True)
-                if for_near:
-                    vals[at : at + 1] = row_value
-                if for_far:
-                    zb[tail + at : tail + at + 1] = row_value
+
+    @pl.when(owner)
+    def _():
+        loads[fields].wait()
+        for slot, f, for_near, for_far in picks:
+            for i in range(per):
+                start = pl.multiple_of(f * per_face + i * width, width)
+                piece = block[:, pl.ds(start, width)]
+                for t in range(steps):
+                    at = (t * VALUE_FACES + slot) * per + i
+                    row_value = jnp.sum(columns[t] * piece, axis=0, keepdims=True)
+                    if for_near:
+                        vals[at : at + 1] = row_value
+                    if for_far:
+                        zb[tail + at : tail + at + 1] = row_value
+
+    @pl.when(~owner)
+    def _():
+        vals[...] = jnp.zeros(vals.shape, F32)
+        zb[tail:] = jnp.zeros(vals.shape, F32)
+
     loads[fields + 1].wait()
 
 

time: 19.6 us -> 19.5 us (level)
  the two profiles are of different devices: /device:TPU:19 before, /device:TPU:21 now
where the time goes in v4:
time: 19.5 us; the launch traced here: 19.3 us
  waiting for transfers between devices  6.75 us (35%)
  starting transfers between devices  6.07 us (31%)
  Pallas kernels  5.2 us (27%)
  between operations  1.32 us (7%)
    ppermute x4, starting transfers between devices, over_slab(): return lax.ppermute(x, 'slab', list(enumerate(partner)))  4.77 us
    ppermute x2, waiting for transfers between devices, over_box(): return lax.ppermute(x, ('box', 'slab'), pairs)  3.64 us
    ppermute x4, waiting for transfers between devices, over_slab(): return lax.ppermute(x, 'slab', list(enumerate(partner)))  3.12 us
    pallas_call x1, Pallas kernels, on_device(): pl.pallas_call(functools.partial(main_kernel, boxes, slabs, len(others)),...  1.75 us
    pallas_call x1, Pallas kernels, on_device(): pl.pallas_call(functools.partial(pack_kernel, slots, slabs), out_shape=(i...  1.6 us
    ppermute x2, starting transfers between devices, over_box(): return lax.ppermute(x, ('box', 'slab'), pairs)  1.3 us
    pallas_call x1, Pallas kernels, on_device(): pl.pallas_call(functools.partial(local_kernel, boxes, slabs, total_z), ou...  1 us
    pallas_call x1, Pallas kernels, on_device(): pl.pallas_call(functools.partial(fix_kernel, boxes, slabs), out_shape=(pl...  0.83 us
  transfers between devices with their start and end apart: 6, of which 4 were waited for; matrix products, arithmetic and copies ran while one was open for 0% of the time, Pallas kernels for 14%

profile of v4, /device:TPU:21, one launch (start us, length us, event | category | flops | bytes accessed | tf_op | source)
XLA Modules:
  0.0 19.3 jit_solution(1291227111506056259)
XLA Ops:
  1.3 1.6 %pack.1 = (f32[2,2,16,16,128]{4,3,2,1,0:T(8,128)S(1)}, f32[2,2,16,16,128]{4,3,2,1,0:T(8,128)S(1)}, f32[2,16,16,128]{3,2,1,0:T(8,128)S(1)}, s32[6,1024]{1,0:T(8,1...) custom-call(s32[1]{0:T(128)S(6)} %copy.13.home, ...), custom_call_target="tpu_custom_call" | custom-call | tf_op jit(solution)/shard_map/pack/pallas_call | solution.py:527
  2.9 1.8 %collective-permute-start.2 = (f32[112,256]{1,0:T(8,128)S(1)}, f32[112,256]{1,0:T(8,128)S(1)}, u32[]{:S(2)}, u32[]{:S(2)}) collective-permute-start(f32[112,256]{1,0:T(8,128)S(1)} %get-tuple-element.28), channel_id=1, source_target_pairs={{0,3},{1,2},{2,1},{3,0},{4,7},{5,6},{6,5},{7,4},{8,11},{9,10},{10,... | collective-permute-start | bytes 344072 | tf_op jit(solution)/shard_map/ppermute | solution.py:511
  4.7 1.0 %local.1 = (f32[2,2,16,16,128]{4,3,2,1,0:T(8,128)S(1)}, bf16[2,256,1024]{2,1,0:T(8,128)(2,1)S(1)}, bf16[2,32,1024]{2,1,0:T(8,128)(2,1)S(1)}, bf16[32,1024]{1,0:T(8,128)(2,1)S(1)}, bf16[3,32,1024]{2,1,0:T(8,128)(2,1)S(1)}) custom-call(f32[2,16,128]{2,1,0:T(8,128)S(1)} %get-tuple-element.29.planes, s32[6,1024]{1,0:T(8,128)S(1)} %get-tuple-element.30.cells, ...), custom_call_target="tpu_custom_call" | custom-call | tf_op jit(solution)/shard_map/local/pallas_call | solution.py:573
  5.7 2.9 %collective-permute-done.2.zb = f32[112,256]{1,0:T(8,128)S(1)} collective-permute-done((f32[112,256]{1,0:T(8,128)S(1)}, f32[112,256]{1,0:T(8,128)S(1)}, u32[]{:S(2)}, u32[]{:S(2)}) %collective-permute-start.2) | collective-permute-done | bytes 114720 | tf_op jit(solution)/shard_map/ppermute | solution.py:511
  8.7 0.5 %collective-permute-start.5 = (f32[112,256]{1,0:T(8,128)S(1)}, f32[112,256]{1,0:T(8,128)S(1)}, u32[]{:S(2)}, u32[]{:S(2)}) collective-permute-start(f32[112,256]{1,0:T(8,128)S(1)} %relay.1.after), channel_id=1, source_target_pairs={{0,1},{1,0},{2,3},{3,2},{4,5},{5,4},{6,7},{7,6},{8,9},{9,8},{10,11... | collective-permute-start | bytes 344072 | tf_op jit(solution)/shard_map/ppermute | solution.py:511
  9.2 1.3 %collective-permute-start = (f32[80,256]{1,0:T(8,128)S(1)}, f32[80,256]{1,0:T(8,128)S(1)}, u32[]{:S(2)}, u32[]{:S(2)}) collective-permute-start(f32[80,256]{1,0:T(8,128)S(1)} %get-tuple-element.24), channel_id=1, source_target_pairs={{0,4},{1,5},{2,6},{3,7},{4,0},{5,1},{6,2},{7,3},{8,12},{9,13},{10,... | collective-permute-start | bytes 245768 | tf_op jit(solution)/shard_map/ppermute | solution.py:523
  10.5 0.0 collective-permute-start.1
  10.5 2.6 %collective-permute-done.xa = f32[80,256]{1,0:T(8,128)S(1)} collective-permute-done((f32[80,256]{1,0:T(8,128)S(1)}, f32[80,256]{1,0:T(8,128)S(1)}, u32[]{:S(2)}, u32[]{:S(2)}) %collective-permute-start) | collective-permute-done | bytes 81952 | tf_op jit(solution)/shard_map/ppermute | solution.py:523
  13.1 1.0 %collective-permute-done.1.xb = f32[80,256]{1,0:T(8,128)S(1)} collective-permute-done((f32[80,256]{1,0:T(8,128)S(1)}, f32[80,256]{1,0:T(8,128)S(1)}, u32[]{:S(2)}, u32[]{:S(2)}) %collective-permute-start.1) | collective-permute-done | bytes 81952 | tf_op jit(solution)/shard_map/ppermute | solution.py:523
  14.2 1.3 %collective-permute-start.3 = (f32[8,256]{1,0:T(8,128)S(1)}, f32[8,256]{1,0:T(8,128)S(1)}, u32[]{:S(2)}, u32[]{:S(2)}) collective-permute-start(f32[8,256]{1,0:T(8,128)S(1)} %get-tuple-element.35), channel_id=1, source_target_pairs={{0,1},{1,0},{2,3},{3,2},{4,5},{5,4},{6,7},{7,6},{8,9},{9,8},{10,11... | collective-permute-start | bytes 24584 | tf_op jit(solution)/shard_map/ppermute | solution.py:511
  15.4 1.1 %collective-permute-start.4 = (f32[8,256]{1,0:T(8,128)S(1)}, f32[8,256]{1,0:T(8,128)S(1)}, u32[]{:S(2)}, u32[]{:S(2)}) collective-permute-start(f32[8,256]{1,0:T(8,128)S(1)} %get-tuple-element.36), channel_id=1, source_target_pairs={{0,3},{1,2},{2,1},{3,0},{4,7},{5,6},{6,5},{7,4},{8,11},{9,10},{10,... | collective-permute-start | bytes 24584 | tf_op jit(solution)/shard_map/ppermute | solution.py:511
  16.5 0.0 collective-permute-done.5.za
  16.6 1.8 %main.1 = (f32[2,16,16,256]{3,2,1,0:T(8,128)}, f32[2,2,16,16,128]{4,3,2,1,0:T(8,128)S(1)}, f32[2,2,16,16,128]{4,3,2,1,0:T(8,128)S(1)}, f32[8,256]{1,0:T(8,128)S(1)}) custom-call(f32[2,16,128]{2,1,0:T(8,128)S(1)} %get-tuple-element.29.planes, f32[4,128]{1,0:T(4,128)S(1)} %get-tuple-element.37.edges, bf16[2,256,1024]{2,1,0:T(8,128)(2,1)S(1)} %get-tuple-element.38.wide, ...), custom_call_target="tpu_custom_call" | custom-call | tf_op jit(solution)/shard_map/main/pallas_call | solution.py:610
  18.3 0.0 collective-permute-done.3.ca
  18.3 0.2 collective-permute-done.4.cb
  18.5 0.8 %fix.1 = (f32[2,16,16,256]{3,2,1,0:T(8,128)}, f32[2,16,16,256]{3,2,1,0:T(8,128)}) custom-call(f32[8,256]{1,0:T(8,128)S(1)} %collective-permute-done.3.ca, f32[8,256]{1,0:T(8,128)S(1)} %collective-permute-done.4.cb, f32[2,2,16,16,128]{4,3,2,1,0:T(8,128)S(1)} %get-tuple-element.42.one, ...), custom_call_target="tpu_custom_call", output_to_operand_aliasing={{1}: (5, {})} | custom-call | tf_op jit(solution)/shard_map/fix/pallas_call | solution.py:634
  (2 shorter events, 0.0 us)
Async XLA Ops:
  2.9 5.8 %collective-permute-start.2 = (f32[112,256]{1,0:T(8,128)S(1)}, f32[112,256]{1,0:T(8,128)S(1)}, u32[]{:S(2)}, u32[]{:S(2)}) collective-permute-start(f32[112,256]{1,0:T(8,128)S(1)} %get-tuple-element.28), channel_id=1, source_target_pairs={{0,3},{1,2},{2,1},{3,0},{4,7},{5,6},{6,5},{7,4},{8,11},{9,10},{10,... | collective-permute-start | bytes 344072 | tf_op jit(solution)/shard_map/ppermute | solution.py:511
  8.7 7.9 %collective-permute-start.5 = (f32[112,256]{1,0:T(8,128)S(1)}, f32[112,256]{1,0:T(8,128)S(1)}, u32[]{:S(2)}, u32[]{:S(2)}) collective-permute-start(f32[112,256]{1,0:T(8,128)S(1)} %relay.1.after), channel_id=1, source_target_pairs={{0,1},{1,0},{2,3},{3,2},{4,5},{5,4},{6,7},{7,6},{8,9},{9,8},{10,11... | collective-permute-start | bytes 344072 | tf_op jit(solution)/shard_map/ppermute | solution.py:511
  9.2 3.9 %collective-permute-start = (f32[80,256]{1,0:T(8,128)S(1)}, f32[80,256]{1,0:T(8,128)S(1)}, u32[]{:S(2)}, u32[]{:S(2)}) collective-permute-start(f32[80,256]{1,0:T(8,128)S(1)} %get-tuple-element.24), channel_id=1, source_target_pairs={{0,4},{1,5},{2,6},{3,7},{4,0},{5,1},{6,2},{7,3},{8,12},{9,13},{10,... | collective-permute-start | bytes 245768 | tf_op jit(solution)/shard_map/ppermute | solution.py:523
  10.5 3.6 %collective-permute-start.1 = (f32[80,256]{1,0:T(8,128)S(1)}, f32[80,256]{1,0:T(8,128)S(1)}, u32[]{:S(2)}, u32[]{:S(2)}) collective-permute-start(f32[80,256]{1,0:T(8,128)S(1)} %get-tuple-element.25), channel_id=1, source_target_pairs={{0,1},{1,0},{2,3},{3,2},{4,8},{5,9},{6,10},{7,11},{8,4},{9,5},{10,... | collective-permute-start | bytes 245768 | tf_op jit(solution)/shard_map/ppermute | solution.py:523
  14.2 4.2 %collective-permute-start.3 = (f32[8,256]{1,0:T(8,128)S(1)}, f32[8,256]{1,0:T(8,128)S(1)}, u32[]{:S(2)}, u32[]{:S(2)}) collective-permute-start(f32[8,256]{1,0:T(8,128)S(1)} %get-tuple-element.35), channel_id=1, source_target_pairs={{0,1},{1,0},{2,3},{3,2},{4,5},{5,4},{6,7},{7,6},{8,9},{9,8},{10,11... | collective-permute-start | bytes 24584 | tf_op jit(solution)/shard_map/ppermute | solution.py:511
  15.4 3.1 %collective-permute-start.4 = (f32[8,256]{1,0:T(8,128)S(1)}, f32[8,256]{1,0:T(8,128)S(1)}, u32[]{:S(2)}, u32[]{:S(2)}) collective-permute-start(f32[8,256]{1,0:T(8,128)S(1)} %get-tuple-element.36), channel_id=1, source_target_pairs={{0,3},{1,2},{2,1},{3,0},{4,7},{5,6},{6,5},{7,4},{8,11},{9,10},{10,... | collective-permute-start | bytes 24584 | tf_op jit(solution)/shard_map/ppermute | solution.py:511
